TPU v7x, 128 devices: a whole 4x4x4 slice. The times are simulated.
128 devices in a mesh: seq: 2 (over core), depth: 2 (over z_hi), vocab: 32 (over z_lo, y, x).
Axes of the slice: x: 4, y: 4, z: 4 (z_hi: 2, z_lo: 2; z = z_hi * 2 + z_lo), core: 2. Of those that a mesh axis runs over, the one named last changes fastest.
Arguments:
- hidden: bfloat16 [2, 512, 7168], P('depth', ('seq', 'vocab')), may hold values from -24 to 24
- embedding: bfloat16 [64640, 7168], P(('seq', 'vocab')), may hold values from -1 to 1
- targets: int32 [2, 512], P('depth', ('seq', 'vocab')), may hold values from 0 to 64639
- mask: int32 [2, 512], P('depth', ('seq', 'vocab')), may hold values 0 or 1
Outputs:
- nll: float32 [2, 512], P('depth', ('seq', 'vocab'))
- loss: float32 [], replicated
- grad_norm: float32 [], replicated
All inputs are finite; a program needn't handle non-finite values. No bound on the sum of `mask` on one device may be relied on, other than what follows from the above.
Results may differ from a plain program's by a relative error of at most 0.0023.
Values may be sent and summed in bfloat16 or wider, within the bound.
A program may use at most 128 MiB of HBM per device.

v0:
```python
import jax
import jax.numpy as jnp
from jax import lax
from jax.sharding import Mesh
from jax.sharding import PartitionSpec as P

SEQ_VOCAB = ("seq", "vocab_0", "vocab_1", "vocab_2")
SEQ_DEPTH_VOCAB = ("seq", "depth", "vocab_0", "vocab_1", "vocab_2")


def sent_together(arrays, axis, dim, along):
    widths = [a.shape[along] for a in arrays]
    both = jnp.concatenate(arrays, axis=along)
    out = lax.all_gather(both, axis, axis=dim, tiled=True)
    return tuple(jnp.split(out, [sum(widths[:k]) for k in range(1, len(widths))], axis=along))


def sent_to_all(shard, axis):
    count = lax.axis_size(axis)
    return lax.all_to_all(
        jnp.broadcast_to(shard[None], (count, *shard.shape)), axis, 0, 0, tiled=True
    )


def all_in_one(shard, axis):
    leaves = jax.tree.leaves(shard)
    turns = sorted(range(len(leaves)), key=lambda k: -leaves[k].size)
    width = (1, *leaves[turns[0]].shape)[-1]
    lines = [
        jnp.pad(leaves[k].reshape(-1), (0, -leaves[k].size % width)).reshape(-1, width)
        for k in turns
    ]
    both, at, found = (sent_to_all(jnp.concatenate(lines), axis), 0, {})
    for k, line in zip(turns, lines):
        slab = both[:, at : at + len(line)].reshape(len(both), -1)
        found[k] = slab[:, : leaves[k].size].reshape(-1, *leaves[k].shape)
        at += len(line)
    numbers = iter(range(len(leaves)))
    return jax.tree.map(lambda _: found[next(numbers)], shard)


def combined_pairwise(pieces, combine):
    while len(jax.tree.leaves(pieces)[0]) > 1:
        pieces = jax.vmap(combine)(
            *(jax.tree.map(lambda part: part[side::2], pieces) for side in (0, 1))
        )
    return jax.tree.map(lambda part: part[0], pieces)


def joined_all(shard, axis, combine):
    pieces = all_in_one(shard, axis)
    return combined_pairwise(pieces, combine)


def taken_together(shard, axis):
    everything = sent_to_all(shard, axis)
    return jnp.sum(everything, axis=0)


def swapped(value, axis, apart):
    mask = 2**apart
    pairs = [(source, source ^ mask) for source in range(lax.axis_size(axis))]
    return lax.ppermute(value, axis, pairs)


def one_axis_at_a_time(shard, axes):
    for axis in axes:
        shard = lax.psum(shard, axis)
    return shard


def combine_stats(first, second):
    peak = jnp.maximum(first[0], second[0])
    total = first[1] * jnp.exp(first[0] - peak) + second[1] * jnp.exp(second[0] - peak)
    return (peak, total, first[2] + second[2])


def rows_product(grad_rows, states):
    part = lax.dot_general(
        grad_rows, states, (((0,), (0,)), ((), ())), preferred_element_type=jnp.float32
    )
    return part


def local(hidden, embedding, targets, mask):
    states, picks, flags = (
        lax.all_gather(hidden, SEQ_VOCAB, axis=1, tiled=True),
        *sent_together((targets, mask), SEQ_VOCAB, 1, 0),
    )
    states = states[0]
    picks = picks[0]
    live = flags[0].astype(jnp.float32)
    width = embedding.shape[0]
    offset = lax.axis_index(SEQ_VOCAB) * width
    logits = lax.dot_general(
        states, embedding, (((1,), (1,)), ((), ())), preferred_element_type=jnp.float32
    )
    ids = offset + lax.broadcasted_iota(jnp.int32, (1, width), 1)
    onehot = picks[:, None] == ids
    local_peak = jnp.max(logits, axis=1)
    chosen = jnp.sum(jnp.where(onehot, logits, jnp.zeros((), jnp.float32)), axis=1)
    part_total = jnp.sum(jnp.exp(logits - local_peak[:, None]), axis=1)
    peak, total, target = joined_all((local_peak, part_total, chosen), SEQ_VOCAB, combine_stats)
    lse = peak + jnp.log(total)
    nll = lse - target
    side = lax.axis_index("depth")
    weight = jnp.where(side == 0, jnp.float32(1.0), jnp.float32(0.3))
    coef = weight / jnp.maximum(jnp.sum(live), jnp.float32(1.0))
    loss = taken_together(coef * jnp.sum(live * nll), "depth")
    grad_rows = (
        coef * live[:, None] * (jnp.exp(logits - lse[:, None]) - onehot.astype(jnp.float32))
    ).astype(jnp.bfloat16)
    half = width // 2
    mine = lax.dynamic_slice_in_dim(grad_rows, side * half, half, 1)
    other = lax.dynamic_slice_in_dim(grad_rows, (1 - side) * half, half, 1)
    recv_grad, recv_states = swapped((other, states), "depth", 0)
    own_part = rows_product(mine, states).astype(jnp.bfloat16)
    peer_part = rows_product(recv_grad, recv_states).astype(jnp.bfloat16)
    own_part, peer_part = lax.optimization_barrier((own_part, peer_part))
    summed = own_part.astype(jnp.float32) + peer_part.astype(jnp.float32)
    square = jnp.sum(summed * summed)
    grad_norm = jnp.sqrt(one_axis_at_a_time(square, SEQ_DEPTH_VOCAB))
    count = hidden.shape[1]
    start = lax.axis_index(SEQ_VOCAB) * count
    nll_own = lax.dynamic_slice_in_dim(nll, start, count, 0)[None, :]
    return (nll_own, loss, grad_norm)


def solution(mesh):
    torus = Mesh(
        mesh.devices.reshape(mesh.shape["seq"], mesh.shape["depth"], 2, 4, 4),
        ("seq", "depth", "vocab_0", "vocab_1", "vocab_2"),
    )
    placed = (
        P("depth", SEQ_VOCAB, None),
        P(SEQ_VOCAB, None),
        P("depth", SEQ_VOCAB),
        P("depth", SEQ_VOCAB),
    )
    return jax.shard_map(
        local,
        mesh=torus,
        in_specs=placed,
        out_specs=(P("depth", SEQ_VOCAB), P(), P()),
        check_vma=False,
    )
```

profile of v0, /device:TPU:1, one launch (start us, length us, event | category | flops | bytes accessed | tf_op | source)
XLA Modules:
  0.0 386.5 jit_solution(1622564863322329766)
XLA Ops:
  7.2 0.0 all-gather.3.cloned.1.call-start
  7.2 0.7 all-gather.3.cloned.1.call-update
  7.9 114.5 %all-gather.3.cloned.1.call-done = bf16[1,512,7168]{2,1,0:T(8,128)(2,1)} async-done(((bf16[1,8,7168]{2,1,0:T(8,128)(2,1)}), bf16[1,512,7168]{2,1,0:T(8,128)(2,1)}) %all-gather.3.cloned.1.call-update) | async-done | bytes 7340048 | tf_op jit(solution)/shard_map/all_gather | solution.py:87
  122.4 2.2 collective-permute-start.1
  124.7 0.7 add_bitcast_fusion
  125.3 139.0 %all-gather = s32[64,8,2]{1,2,0:T(2,128)S(1)} all-gather(s32[1,8,2]{1,2,0:T(2,128)S(1)} %add_bitcast_fusion), channel_id=1, replica_groups=mesh['seq'=2,'depth'=2,'vocab_0'=2,'vocab_1'=4,'vocab_2'=4] {'seq','voca..., dimensions={0}, use_global_device_ids=true | all-gather | bytes 4160 | tf_op jit(solution)/shard_map/all_gather | solution.py:14
  264.3 0.1 reshape.62
  264.5 13.0 %fusion.14 = (f32[512]{0:T(512)S(1)}, f32[512,1010]{0,1:T(8,128)S(1)}) fusion(bf16[1010,7168]{1,0:T(8,128)(2,1)} %param.5, bf16[1,512,7168]{2,1,0:T(8,128)(2,1)} %all-gather.3.cloned.1.call-done), kind=kOutput, calls=%fused_computation.41 | convolution fusion | flops 7413948928 | bytes 23889920 | tf_op jit(solution)/shard_map/dot_general | solution.py:95
  277.5 0.5 exponential_reduce_fusion
  278.0 0.9 broadcast_in_dim.11
  278.9 18.0 %all-to-all-start = ((f32[64,3,512]{2,1,0:T(4,128)}), f32[64,3,512]{2,1,0:T(4,128)S(1)}, u32[]{:S(2)}, u32[]{:S(2)}) async-start(f32[64,3,512]{2,1,0:T(4,128)} %broadcast_in_dim.11), calls=%async_computation | async-start | bytes 1048576 | tf_op jit(solution)/shard_map/all_to_all | solution.py:20
  297.0 0.6 fusion.11
  298.3 11.3 %all-to-all-done = f32[64,3,512]{2,1,0:T(4,128)S(1)} async-done(((f32[64,3,512]{2,1,0:T(4,128)}), f32[64,3,512]{2,1,0:T(4,128)S(1)}, u32[]{:S(2)}, u32[]{:S(2)}) %all-to-all-start) | async-done | bytes 393248 | tf_op jit(solution)/shard_map/all_to_all | solution.py:20
  309.6 0.3 fusion.12
  310.9 0.6 multiply_reduce_fusion.1
  311.5 0.5 fusion.3
  312.0 0.1 constant_dynamic-slice_fusion
  312.1 0.8 collective-permute-start
  312.9 7.3 %convolution_convert_fusion.1 = bf16[505,7168]{1,0:T(8,128)(2,1)S(1)} fusion(bf16[512,1010]{0,1:T(8,128)(2,1)S(1)} %fusion.3, s32[]{:T(128)S(6)} %select_n.20, bf16[1,512,7168]{2,1,0:T(8,128)(2,1)} %all-gather.3.cloned.1.call-done), kind=kOutput, calls=%fused_computation.2 | convolution fusion | flops 3710336000 | bytes 15104004 | tf_op jit(solution)/shard_map/dot_general | solution.py:79
  320.2 6.9 %collective-permute-done = bf16[512,505]{0,1:T(8,128)(2,1)S(1)} collective-permute-done((bf16[512,505]{0,1:T(8,128)(2,1)S(1)}, bf16[512,505]{0,1:T(8,128)(2,1)S(1)}, u32[]{:S(2)}, u32[]{:S(2)}) %collective-permute-start) | collective-permute-done | bytes 517152 | tf_op jit(solution)/shard_map/ppermute | solution.py:63
  327.1 0.0 collective-permute-done.1
  327.1 9.3 %convolution_convert_fusion = bf16[505,7168]{1,0:T(8,128)(2,1)} fusion(bf16[512,505]{0,1:T(8,128)(2,1)S(1)} %collective-permute-done, bf16[512,7168]{1,0:T(8,128)(2,1)} %collective-permute-done.1), kind=kOutput, calls=%fused_computation.1 | convolution fusion | flops 3710336000 | bytes 15096832 | tf_op jit(solution)/shard_map/dot_general | solution.py:79
  336.4 7.5 %multiply_reduce_fusion = f32[]{:T(128)} fusion(bf16[505,7168]{1,0:T(8,128)(2,1)} %convolution_convert_fusion, bf16[505,7168]{1,0:T(8,128)(2,1)S(1)} %convolution_convert_fusion.1), kind=kLoop, calls=%fused_computation | loop fusion | flops 18099200 | bytes 14479364 | tf_op jit(solution)/shard_map/reduce_sum | solution.py:121
  343.9 3.8 psum.35
  348.4 5.9 %psum.36 = f32[]{:T(128)} all-reduce(f32[]{:T(128)} %psum.35), channel_id=1, replica_groups=mesh['seq'=2,'depth'=2,'vocab_0'=2,'vocab_1'=4,'vocab_2'=4] {'depth'}, use_global_device_ids=true, to_apply=%region_8.9 | all-reduce | flops 1 | bytes 8 | tf_op jit(solution)/shard_map/psum | solution.py:68
  354.3 0.6 broadcast_in_dim.13
  354.9 3.2 all-to-all-start.1
  358.2 4.4 %psum.37 = f32[]{:T(128)} all-reduce(f32[]{:T(128)} %psum.36), channel_id=1, replica_groups=mesh['seq'=2,'depth'=2,'vocab_0'=2,'vocab_1'=4,'vocab_2'=4] {'vocab_0'}, use_global_device_ids=true, to_apply=%region_9.10 | all-reduce | flops 1 | bytes 8 | tf_op jit(solution)/shard_map/psum | solution.py:68
  362.6 0.6 dynamic-slice_bitcast_fusion
  363.2 6.9 %psum.38 = f32[]{:T(128)} all-reduce(f32[]{:T(128)} %psum.37), channel_id=1, replica_groups=mesh['seq'=2,'depth'=2,'vocab_0'=2,'vocab_1'=4,'vocab_2'=4] {'vocab_1'}, use_global_device_ids=true, to_apply=%region_10.11 | all-reduce | flops 1 | bytes 8 | tf_op jit(solution)/shard_map/psum | solution.py:68
  370.1 0.0 all-to-all-done.1
  370.1 0.6 reduce_sum.58
  370.7 7.2 %psum.39 = f32[]{:T(128)} all-reduce(f32[]{:T(128)} %psum.38), channel_id=1, replica_groups=mesh['seq'=2,'depth'=2,'vocab_0'=2,'vocab_1'=4,'vocab_2'=4] {'vocab_2'}, use_global_device_ids=true, to_apply=%region_11.12 | all-reduce | flops 1 | bytes 8 | tf_op jit(solution)/shard_map/psum | solution.py:68
  (48 shorter events, 0.9 us)
Async XLA Ops:
  7.2 115.3 %all-gather.3.cloned.1.call-start = ((), (), s32[]{:S(2)}) async-start(), calls=%async_computation.2 | async-start | bytes 7454720 | tf_op jit(solution)/shard_map/all_gather | solution.py:87
  122.4 204.7 %collective-permute-start.1 = (bf16[512,7168]{1,0:T(8,128)(2,1)}, bf16[512,7168]{1,0:T(8,128)(2,1)}, u32[]{:S(2)}, u32[]{:S(2)}) collective-permute-start(bf16[512,7168]{1,0:T(8,128)(2,1)} %bitcast.46), channel_id=1, source_target_pairs={{0,32},{32,0},{1,33},{33,1},{2,34},{34,2},{3,35},{35,3},{4,36},{36... | collective-permute-start | bytes 22020104 | tf_op jit(solution)/shard_map/ppermute | solution.py:63
  278.9 30.7 %all-to-all-start = ((f32[64,3,512]{2,1,0:T(4,128)}), f32[64,3,512]{2,1,0:T(4,128)S(1)}, u32[]{:S(2)}, u32[]{:S(2)}) async-start(f32[64,3,512]{2,1,0:T(4,128)} %broadcast_in_dim.11), calls=%async_computation | async-start | bytes 1048576 | tf_op jit(solution)/shard_map/all_to_all | solution.py:20
  312.1 15.0 %collective-permute-start = (bf16[512,505]{0,1:T(8,128)(2,1)S(1)}, bf16[512,505]{0,1:T(8,128)(2,1)S(1)}, u32[]{:S(2)}, u32[]{:S(2)}) collective-permute-start(bf16[512,505]{0,1:T(8,128)(2,1)S(1)} %constant_dynamic-slice_fusion), channel_id=1, source_target_pairs={{0,32},{32,0},{1,33},{33,1},{2,34},{34,2},{3,35},{35,3},{4,36},{36... | collective-permute-start | bytes 1551368 | tf_op jit(solution)/shard_map/ppermute | solution.py:63
  354.9 15.1 %all-to-all-start.1 = ((f32[2,1,1]{2,1,0:T(1,128)}), f32[2,1,1]{2,1,0:T(1,128)S(1)}, u32[]{:S(2)}, u32[]{:S(2)}) async-start(f32[2,1,1]{2,1,0:T(1,128)} %broadcast_in_dim.13), calls=%async_computation.1 | async-start | bytes 2048 | tf_op jit(solution)/shard_map/all_to_all | solution.py:20
Sparse Core Ops, SparseCore 0:
  9.7 112.7 all-gather.2
where the time goes:
time: 392 us; the launch traced here: 387 us
  blocking collectives  167 us (43%)
  waiting for transfers between devices  134 us (34%)
  matrix products  29.6 us (8%)
  starting transfers between devices  24.3 us (6%)
  between operations  17.4 us (4%)
  other arithmetic  11.2 us (3%)
    all_gather x1, blocking collectives, sent_together(): out = lax.all_gather(both, axis, axis=dim, tiled=True)  139 us
    all_gather x1, waiting for transfers between devices, local(): lax.all_gather(hidden, SEQ_VOCAB, axis=1, tiled=True)  115 us
    psum x5, blocking collectives, one_axis_at_a_time(): shard = lax.psum(shard, axis)  28.3 us
    all_to_all x2, starting transfers between devices, sent_to_all(): lax.all_to_all(jnp.broadcast_to(shard[None], (count, *shard.shape)), axis...  21.2 us
    dot_general x2, matrix products, rows_product(): lax.dot_general(grad_rows, states, (((0,), (0,)), ((), ())), preferred_el...  16.6 us
    dot_general x1, matrix products, local(): lax.dot_general(states, embedding, (((1,), (1,)), ((), ())), preferred_el...  13 us
    all_to_all x2, waiting for transfers between devices, sent_to_all(): lax.all_to_all(jnp.broadcast_to(shard[None], (count, *shard.shape)), axis...  11.3 us
  transfers between devices with their start and end apart: 5, of which 3 were waited for; matrix products, arithmetic and copies ran while one was open for 7% of the time, Pallas kernels for 0%

commit v1 on v0

v1 whole, which is shorter than its diff:
```python
import functools

import jax
import jax.numpy as jnp
from jax import lax
from jax.experimental import pallas as pl
from jax.experimental.pallas import tpu as pltpu
from jax.sharding import Mesh
from jax.sharding import PartitionSpec as P

MESH = pl.DeviceIdType.MESH
F32 = jnp.float32
BF16 = jnp.bfloat16

VOC = 1010
VPAD = 1024
D = 7168
T = 512
SLICES = 7
WIDTH = D // SLICES
SUBS = 4
SUBW = WIDTH // SUBS
STEPS = 4
NEUTRAL = -1e30
SHIFT = 13.862943611198906
CYCLE = (5, 3, 4, 2)


def kernel(
    hid_ref, emb_ref, tgt_ref, mask_ref, out_ref,
    h, emb, hp, l, b, x, xall, w, wp, ep, y, yx,
    ints1, ints2, st1, st2, fin1, fin2, live_buf, cols_buf,
    hid_sem, emb_sem, hs, hr, xs, xr, hps, hpr, es, er,
    is1, ir1, is2, ir2, ss1, sr1, ss2, sr2, fs1, fr1, fs2, fr2,
):
    ms, md, mz, my, mx = (lax.axis_index(a) for a in ("s", "d", "zl", "y", "x"))
    zz = md * 2 + mz
    qx1, qx0 = mx // 2, (mx + mx // 2) % 2
    qy1, qy0 = my // 2, (my + my // 2) % 2
    mine = (ms, mz, qy1, qy0, qx1, qx0)
    partner = {
        5: {"x": mx + 1 - 2 * (mx % 2)},
        4: {"x": 3 - mx},
        3: {"y": my + 1 - 2 * (my % 2)},
        2: {"y": 3 - my},
        1: {"zl": 1 - mz},
        0: {"s": 1 - ms},
    }
    item = ((((ms * 2 + mz) * 2 + qy1) * 2 + qy0) * 2 + qx1) * 2 + qx0
    col_id = ms * 4 + zz
    plane_id = my * 4 + mx

    def col_peer(k):
        s = (ms + k // 4) % 2
        z = (zz + k % 4) % 4
        return s * 4 + z, {"s": s, "d": z // 2, "zl": z % 2}

    def plane_peer(k):
        yy = (my + k // 4) % 4
        xx = (mx + k % 4) % 4
        return yy * 4 + xx, {"y": yy, "x": xx}

    own = pltpu.make_async_copy(hid_ref.at[0], h.at[mine], hid_sem)
    own.start()

    def emb_copy(c):
        cs = pl.ds(pl.multiple_of(c * WIDTH, WIDTH), WIDTH)
        return pltpu.make_async_copy(emb_ref.at[:, cs], emb.at[:, cs], emb_sem.at[c])

    barrier = pltpu.get_barrier_semaphore()
    for k in range(1, 8):
        pl.semaphore_signal(barrier, inc=1, device_id=col_peer(k)[1], device_id_type=MESH)
    for k in range(1, 16):
        pl.semaphore_signal(barrier, inc=1, device_id=plane_peer(k)[1], device_id_type=MESH)
    for c in range(SLICES):
        emb_copy(c).start()

    lane = lax.broadcasted_iota(jnp.int32, (8, T), 1)
    row8 = lax.broadcasted_iota(jnp.int32, (8, T), 0)
    ints = jnp.zeros((8, T), jnp.int32)
    for i in range(8):
        here = lane == item * 8 + i
        ints = jnp.where(here & (row8 == md), tgt_ref[0, i], ints)
        ints = jnp.where(here & (row8 == 2 + md), mask_ref[0, i], ints)
    ints1[col_id] = ints
    own.wait()
    pl.semaphore_wait(barrier, 22)

    def sends(buf, my_slot, peer, count, ssem, rsem):
        out = []
        for k in range(1, count):
            _, dev = peer(k)
            out.append(pltpu.make_async_remote_copy(
                src_ref=buf.at[my_slot], dst_ref=buf.at[my_slot],
                send_sem=ssem.at[k], recv_sem=rsem.at[my_slot],
                device_id=dev, device_id_type=MESH))
        return out

    def arrive(buf, peer, count, ssem, rsem):
        for k in range(1, count):
            slot, dev = peer(k)
            pltpu.make_async_remote_copy(
                src_ref=buf.at[slot], dst_ref=buf.at[slot],
                send_sem=ssem.at[k], recv_sem=rsem.at[slot],
                device_id=dev, device_id_type=MESH).wait_recv()

    def box(held, flip, cs):
        index = []
        for dim in range(6):
            if dim in held:
                index.append(slice(None))
            elif dim == flip:
                index.append(1 - mine[dim])
            else:
                index.append(mine[dim])
        return tuple(index) + (slice(None), cs)

    def step_copy(buf, held, dim, cs, ssem, rsem, incoming=False):
        where = buf.at[box(held, dim if incoming else None, cs)]
        return pltpu.make_async_remote_copy(
            src_ref=where, dst_ref=where, send_sem=ssem, recv_sem=rsem,
            device_id=partner[dim], device_id_type=MESH)

    def cube_copy(buf, slots, sub, step, start, width, ssem, rsem, incoming=False):
        dims = [CYCLE[(sub + k) % 4] for k in range(4)]
        held = (1, *dims[:step])
        cs = pl.ds(pl.multiple_of(start + sub * width, width), width)
        k = 1 + sub * STEPS + step
        return step_copy(buf, held, dims[step], cs, ssem.at[(*slots, k)], rsem.at[(*slots, k)], incoming)

    def z_copy(buf, slots, start, width, ssem, rsem, incoming=False):
        cs = pl.ds(pl.multiple_of(start, width), width)
        return step_copy(buf, (), 1, cs, ssem.at[(*slots, 0)], rsem.at[(*slots, 0)], incoming)

    def core_copy(buf, slots, start, width, ssem, rsem, incoming=False):
        cs = pl.ds(pl.multiple_of(start, width), width)
        return step_copy(buf, (1, 2, 3, 4, 5), 0, cs, ssem.at[(*slots, 17)], rsem.at[(*slots, 17)], incoming)

    for c in range(SLICES):
        z_copy(h, (c,), c * WIDTH, WIDTH, hs, hr).start()
    hp_copy = pltpu.make_async_remote_copy(
        src_ref=h.at[mine], dst_ref=hp, send_sem=hps, recv_sem=hpr,
        device_id={"d": 1 - md}, device_id_type=MESH)
    hp_copy.start()
    for copy in sends(ints1, col_id, col_peer, 8, is1, ir1):
        copy.start()

    l[...] = jnp.zeros_like(l)
    b[...] = jnp.zeros_like(b)
    x[...] = jnp.zeros_like(x)
    h2 = h.reshape(T, D)

    def nt(lhs, rhs):
        return lax.dot_general(lhs, rhs, (((1,), (1,)), ((), ())), preferred_element_type=F32)

    def body(i, carry):
        c4 = i - 4

        @pl.when((c4 >= 0) & (c4 < SLICES))
        def _():
            for sub in range(SUBS):
                cube_copy(h, (c4,), sub, 3, c4 * WIDTH, SUBW, hs, hr, True).wait_recv()
            core_copy(h, (c4,), c4 * WIDTH, WIDTH, hs, hr).start()

        for step in (3, 2, 1):
            c = i - step

            @pl.when((c >= 0) & (c < SLICES))
            def _(c=c, step=step):
                for sub in range(SUBS):
                    cube_copy(h, (c,), sub, step - 1, c * WIDTH, SUBW, hs, hr, True).wait_recv()
                    cube_copy(h, (c,), sub, step, c * WIDTH, SUBW, hs, hr).start()

        @pl.when(i < SLICES)
        def _():
            z_copy(h, (i,), i * WIDTH, WIDTH, hs, hr, True).wait_recv()
            for sub in range(SUBS):
                cube_copy(h, (i,), sub, 0, i * WIDTH, SUBW, hs, hr).start()

        @pl.when(i == 3)
        def _():
            hp_copy.wait_recv()
            arrive(ints1, col_peer, 8, is1, ir1)
            ints2[plane_id] = sum(ints1[k] for k in range(8))
            for copy in sends(ints2, plane_id, plane_peer, 16, is2, ir2):
                copy.start()

        c5 = i - 5

        @pl.when(c5 >= 0)
        def _():
            core_copy(h, (c5,), c5 * WIDTH, WIDTH, hs, hr, True).wait_recv()
            emb_copy(c5).wait()
            cs = pl.ds(pl.multiple_of(c5 * WIDTH, WIDTH), WIDTH)

            def half(n, carry):
                ts = pl.ds(pl.multiple_of(n * 256, 256), 256)
                hn = h2[ts, cs]
                l[0:VOC, ts] += nt(emb[:, cs], hn)
                b[:, ts] += nt(h2[:, cs], hn)
                x[:, ts] += nt(hp[:, cs], hn)
                return carry

            lax.fori_loop(0, 2, half, 0)

        return carry

    lax.fori_loop(0, SLICES + 5, body, 0)

    arrive(ints2, plane_peer, 16, is2, ir2)
    ints = sum(ints2[k] for k in range(16))
    first_id = (ms * 32 + mz * 16 + my * 4 + mx) * VOC
    local_t = ints[0:2] - first_id
    local_t = jnp.where(local_t < VOC, local_t, -1)
    own_t = jnp.where(md == 0, local_t[0:1], local_t[1:2])
    other_t = jnp.where(md == 0, local_t[1:2], local_t[0:1])
    live_buf[0:2] = ints[2:4].astype(F32)

    xall[mine] = x[...]
    z_copy(xall, (), 0, T, xs, xr).start()

    tail = l[VOC - 2 : VPAD]
    tail_row = lax.broadcasted_iota(jnp.int32, tail.shape, 0)
    l[VOC - 2 : VPAD] = jnp.where(tail_row < 2, tail, NEUTRAL)
    blk = 64
    groups = blk // 8
    rows = lax.broadcasted_iota(jnp.int32, (blk, T), 0)

    def peak_body(i, carry):
        peak, chosen = carry
        at = pl.multiple_of(i * blk, blk)
        part = l[pl.ds(at, blk)]
        hit = (rows + at) == own_t
        peak = jnp.maximum(peak, jnp.max(part.reshape(groups, 8, T), axis=0))
        chosen = chosen + jnp.sum(jnp.where(hit, part, 0.0).reshape(groups, 8, T), axis=0)
        return peak, chosen

    peak, chosen = lax.fori_loop(
        0, VPAD // blk, peak_body,
        (jnp.full((8, T), NEUTRAL, F32), jnp.zeros((8, T), F32)))
    origin = jnp.max(peak, axis=0, keepdims=True) - SHIFT
    chosen = jnp.sum(chosen, axis=0, keepdims=True)

    def exp_body(i, total):
        at = pl.multiple_of(i * blk, blk)
        e = jnp.exp(l[pl.ds(at, blk)] - origin)
        hit = (rows + at) == own_t
        w[pl.ds(at, blk), 0:T] = jnp.where(hit, 0.0, e).astype(BF16)
        w[pl.ds(at, blk), T : 2 * T] = jnp.where(hit, 1.0, 0.0).astype(BF16)
        return total + jnp.sum(e.reshape(groups, 8, T), axis=0)

    total = lax.fori_loop(0, VPAD // blk, exp_body, jnp.zeros((8, T), F32))
    total = jnp.sum(total, axis=0, keepdims=True)
    stats = jnp.where(row8 < 2, NEUTRAL, jnp.zeros((8, T), F32))
    stats = jnp.where(row8 == md, origin, stats)
    stats = jnp.where(row8 == 2 + md, total, stats)
    stats = jnp.where(row8 == 4 + md, chosen, stats)
    st1[col_id] = stats
    for copy in sends(st1, col_id, col_peer, 8, ss1, sr1):
        copy.start()

    z_copy(xall, (), 0, T, xs, xr, True).wait_recv()
    for sub in range(SUBS):
        cube_copy(xall, (), sub, 0, 0, T // SUBS, xs, xr).start()

    half_rows = VPAD // 2
    theirs = pl.ds(pl.multiple_of((1 - md) * half_rows, half_rows), half_rows)
    ours = pl.ds(pl.multiple_of(md * half_rows, half_rows), half_rows)
    e_copy = pltpu.make_async_remote_copy(
        src_ref=w.at[theirs, pl.ds(0, T)], dst_ref=ep, send_sem=es, recv_sem=er,
        device_id={"d": 1 - md}, device_id_type=MESH)
    e_copy.start()

    def merge(parts):
        top = parts[0][0:2]
        for p in parts[1:]:
            top = jnp.maximum(top, p[0:2])
        tot = jnp.zeros((2, T), F32)
        pick = jnp.zeros((2, T), F32)
        for p in parts:
            tot = tot + p[2:4] * jnp.exp(p[0:2] - top)
            pick = pick + p[4:6]
        return top, tot, pick

    arrive(st1, col_peer, 8, ss1, sr1)
    top, tot, pick = merge([st1[k] for k in range(8)])
    st2[plane_id, 0:2] = top
    st2[plane_id, 2:4] = tot
    st2[plane_id, 4:6] = pick
    st2[plane_id, 6:8] = jnp.zeros((2, T), F32)
    for copy in sends(st2, plane_id, plane_peer, 16, ss2, sr2):
        copy.start()

    for step in (1, 2, 3):
        for sub in range(SUBS):
            cube_copy(xall, (), sub, step - 1, 0, T // SUBS, xs, xr, True).wait_recv()
            cube_copy(xall, (), sub, step, 0, T // SUBS, xs, xr).start()

    gb = 256

    def gram_own(i, carry):
        at = pl.multiple_of(i * gb, gb)
        brow = pl.multiple_of((i % (T // gb)) * gb, gb)
        lhs = w[:, pl.ds(at, gb)]
        bb = b[pl.ds(brow, gb), :]
        for n in range(2):
            part = lax.dot_general(
                lhs, w[:, n * T : (n + 1) * T], (((0,), (0,)), ((), ())),
                preferred_element_type=F32)
            y[pl.ds(at, gb), n * T : (n + 1) * T] = part * bb
        return carry

    lax.fori_loop(0, 2 * T // gb, gram_own, 0)

    def other_hot(i, carry):
        at = pl.multiple_of(i * blk, blk)
        hit = (rows + (at + md * half_rows)) == other_t
        wp[pl.ds(at, blk), T : 2 * T] = jnp.where(hit, 1.0, 0.0).astype(BF16)
        return carry

    lax.fori_loop(0, half_rows // blk, other_hot, 0)

    for sub in range(SUBS):
        cube_copy(xall, (), sub, 3, 0, T // SUBS, xs, xr, True).wait_recv()
    core_copy(xall, (), 0, T, xs, xr).start()

    e_copy.wait_recv()
    wp[:, 0:T] = ep[...]
    core_copy(xall, (), 0, T, xs, xr, True).wait_recv()
    x2 = xall.reshape(T, T)

    def gram_cross(i, carry):
        at = pl.multiple_of(i * gb, gb)
        brow = pl.multiple_of((i % (T // gb)) * gb, gb)
        lhs = wp[:, pl.ds(at, gb)]
        bb = x2[pl.ds(brow, gb), :]
        for n in range(2):
            part = lax.dot_general(
                lhs, w[ours, n * T : (n + 1) * T], (((0,), (0,)), ((), ())),
                preferred_element_type=F32)
            yx[pl.ds(at, gb), n * T : (n + 1) * T] = part * bb
        return carry

    lax.fori_loop(0, 2 * T // gb, gram_cross, 0)

    arrive(st2, plane_peer, 16, ss2, sr2)
    top, tot, pick = merge([st2[k] for k in range(16)])
    lse = top + jnp.log(tot)
    nll = lse - pick
    live = live_buf[0:2]
    weight = jnp.where(lax.broadcasted_iota(jnp.int32, (2, 1), 0) == 0, 1.0, 0.3).astype(F32)
    coef = weight / jnp.maximum(jnp.sum(live, axis=1, keepdims=True), 1.0)
    loss = jnp.sum(coef * jnp.sum(live * nll, axis=1, keepdims=True), axis=0, keepdims=True)
    scale = coef * live
    g = scale * (jnp.exp(pick - lse) - 1.0)
    partner_slot = ms * 4 + (1 - md) * 2 + mz
    origin_p = jnp.where(md == 0, st1[partner_slot, 1:2], st1[partner_slot, 0:1])

    def pair(a):
        return (jnp.where(md == 0, a[0:1], a[1:2]), jnp.where(md == 0, a[1:2], a[0:1]))

    scale_o, scale_p = pair(scale)
    lse_o, lse_p = pair(lse)
    g_o, g_p = pair(g)
    s_o = scale_o * jnp.exp(origin - lse_o)
    s_p = scale_p * jnp.exp(origin_p - lse_p)
    vecs = jnp.where(row8 == 0, s_o, jnp.where(row8 == 1, g_o, jnp.where(row8 == 2, s_p, jnp.where(row8 == 3, g_p, 0.0))))
    cols_buf[...] = vecs.T

    qb = 64

    def quad(i, carry):
        acc_s, acc_g = carry
        at = pl.multiple_of(i * qb, qb)
        cols = cols_buf[pl.ds(at, qb), :]
        at2 = pl.multiple_of(T + at, qb)
        so, go, sp, gp = (cols[:, k : k + 1] for k in range(4))
        sp, gp = 2.0 * sp, 2.0 * gp
        left = (so * y[pl.ds(at, qb), 0:T] + go * y[pl.ds(at2, qb), 0:T]
                + sp * yx[pl.ds(at, qb), 0:T] + gp * yx[pl.ds(at2, qb), 0:T])
        right = (so * y[pl.ds(at, qb), T : 2 * T] + go * y[pl.ds(at2, qb), T : 2 * T]
                 + sp * yx[pl.ds(at, qb), T : 2 * T] + gp * yx[pl.ds(at2, qb), T : 2 * T])
        acc_s = acc_s + jnp.sum(left.reshape(qb // 8, 8, T), axis=0)
        acc_g = acc_g + jnp.sum(right.reshape(qb // 8, 8, T), axis=0)
        return acc_s, acc_g

    zero = jnp.zeros((8, T), F32)
    acc_s, acc_g = lax.fori_loop(0, T // qb, quad, (zero, zero))
    q = jnp.sum(jnp.sum(acc_s * s_o + acc_g * g_o, axis=0, keepdims=True), axis=1, keepdims=True)
    fin1[col_id] = jnp.broadcast_to(q, (8, 128))
    for copy in sends(fin1, col_id, col_peer, 8, fs1, fr1):
        copy.start()

    def drain(c, carry):
        z_copy(h, (c,), c * WIDTH, WIDTH, hs, hr).wait_send()
        for sub in range(SUBS):
            for step in range(STEPS):
                cube_copy(h, (c,), sub, step, c * WIDTH, SUBW, hs, hr).wait_send()
        core_copy(h, (c,), c * WIDTH, WIDTH, hs, hr).wait_send()
        return carry

    lax.fori_loop(0, SLICES, drain, 0)
    z_copy(xall, (), 0, T, xs, xr).wait_send()
    for sub in range(SUBS):
        for step in range(STEPS):
            cube_copy(xall, (), sub, step, 0, T // SUBS, xs, xr).wait_send()
    core_copy(xall, (), 0, T, xs, xr).wait_send()
    hp_copy.wait_send()
    e_copy.wait_send()
    for args in (
        (ints1, col_id, col_peer, 8, is1, ir1), (ints2, plane_id, plane_peer, 16, is2, ir2),
        (st1, col_id, col_peer, 8, ss1, sr1), (st2, plane_id, plane_peer, 16, ss2, sr2),
    ):
        for copy in sends(*args):
            copy.wait_send()

    arrive(fin1, col_peer, 8, fs1, fr1)
    fin2[plane_id] = sum(fin1[k] for k in range(8))
    last = sends(fin2, plane_id, plane_peer, 16, fs2, fr2)
    for copy in last:
        copy.start()
    arrive(fin2, plane_peer, 16, fs2, fr2)
    norm = jnp.sqrt(jnp.maximum(sum(fin2[k] for k in range(16)), 0.0))
    nll_own, _ = pair(nll)
    out = jnp.where(row8 == 0, nll_own, jnp.where(row8 == 1, loss, norm[0:1, 0:1]))
    out_ref[...] = out
    for copy in sends(fin1, col_id, col_peer, 8, fs1, fr1) + last:
        copy.wait_send()


def local(hidden, embedding, targets, mask):
    dma = pltpu.SemaphoreType.DMA
    out = pl.pallas_call(
        kernel,
        out_shape=jax.ShapeDtypeStruct((8, T), F32),
        in_specs=[
            pl.BlockSpec(memory_space=pl.ANY),
            pl.BlockSpec(memory_space=pl.ANY),
            pl.BlockSpec(memory_space=pltpu.SMEM),
            pl.BlockSpec(memory_space=pltpu.SMEM),
        ],
        out_specs=pl.BlockSpec(memory_space=pltpu.VMEM),
        scratch_shapes=[
            pltpu.VMEM((2, 2, 2, 2, 2, 2, 8, D), BF16),
            pltpu.VMEM((VOC, D), BF16),
            pltpu.VMEM((8, D), BF16),
            pltpu.VMEM((VPAD, T), F32),
            pltpu.VMEM((T, T), F32),
            pltpu.VMEM((8, T), F32),
            pltpu.VMEM((2, 2, 2, 2, 2, 2, 8, T), F32),
            pltpu.VMEM((VPAD, 2 * T), BF16),
            pltpu.VMEM((VPAD // 2, 2 * T), BF16),
            pltpu.VMEM((VPAD // 2, T), BF16),
            pltpu.VMEM((2 * T, 2 * T), F32),
            pltpu.VMEM((2 * T, 2 * T), F32),
            pltpu.VMEM((8, 8, T), jnp.int32),
            pltpu.VMEM((16, 8, T), jnp.int32),
            pltpu.VMEM((8, 8, T), F32),
            pltpu.VMEM((16, 8, T), F32),
            pltpu.VMEM((8, 8, 128), F32),
            pltpu.VMEM((16, 8, 128), F32),
            pltpu.VMEM((8, T), F32),
            pltpu.VMEM((T, 8), F32),
            dma,
            dma((SLICES,)),
            dma((SLICES, 18)),
            dma((SLICES, 18)),
            dma((18,)),
            dma((18,)),
            dma,
            dma,
            dma,
            dma,
            dma((8,)), dma((8,)), dma((16,)), dma((16,)),
            dma((8,)), dma((8,)), dma((16,)), dma((16,)),
            dma((8,)), dma((8,)), dma((16,)), dma((16,)),
        ],
        compiler_params=pltpu.CompilerParams(collective_id=0, has_side_effects=True),
        name="heads",
    )(hidden, embedding, targets, mask)
    ms, mz, my, mx = (lax.axis_index(a) for a in ("s", "zl", "y", "x"))
    item = ((ms * 2 + mz) * 4 + my // 2 * 2 + (my + my // 2) % 2) * 4 + mx // 2 * 2 + (mx + mx // 2) % 2
    nll = lax.dynamic_slice(out, (0, item * 8), (1, 8))
    return (nll, out[1, 0], out[2, 0])


def solution(mesh):
    torus = Mesh(mesh.devices.reshape(2, 2, 2, 4, 4), ("s", "d", "zl", "y", "x"))
    group = ("s", "zl", "y", "x")
    return jax.shard_map(
        local,
        mesh=torus,
        in_specs=(P("d", group, None), P(group, None), P("d", group), P("d", group)),
        out_specs=(P("d", group), P(), P()),
        check_vma=False,
    )
```

time: 392 us -> 102 us (0.26); the launches traced: 387 us -> 102 us
  blocking collectives: 167 us -> 0 us
  waiting for transfers between devices: 134 us -> 0 us
  Pallas kernels: 0 us -> 98.5 us
  matrix products: 29.6 us -> 0 us
  starting transfers between devices: 24.3 us -> 0 us
  between operations: 17.4 us -> 0.71 us
  other arithmetic: 11.2 us -> 0 us
    all_gather x1 -> x0, blocking collectives: 139 us -> none  [sent_together(): out = lax.all_gather(both, axis, axis=dim, tiled=True)]
    all_gather x1 -> x0, waiting for transfers between devices: 115 us -> none  [local(): lax.all_gather(hidden, SEQ_VOCAB, axis=1, tiled=True)]
    pallas_call x0 -> x1, Pallas kernels: none -> 98.5 us  [local(): pl.pallas_call(kernel, out_shape=jax.ShapeDtypeStruct((8, T), F32), in_sp...]
    dot_general x3 -> x0, matrix products: 29.6 us -> none  [the longest x2 16.6 us: rows_product(): lax.dot_general(grad_rows, states, (((0,), (0,)), ((), ())), preferred_el...]
    psum x5 -> x0, blocking collectives: 28.3 us -> none  [one_axis_at_a_time(): shard = lax.psum(shard, axis)]
    all_to_all x2 -> x0, starting transfers between devices: 21.2 us -> none  [sent_to_all(): lax.all_to_all(jnp.broadcast_to(shard[None], (count, *shard.shape)), axis...]
    all_to_all x2 -> x0, waiting for transfers between devices: 11.3 us -> none  [sent_to_all(): lax.all_to_all(jnp.broadcast_to(shard[None], (count, *shard.shape)), axis...]
    reduce_sum x5 -> x0, other arithmetic: 9.8 us -> none  [the longest x1 7.48 us: local(): square = jnp.sum(summed * summed)]
  transfers between devices with their start and end apart: 5 -> 0, of which waited for: 3 -> 0; matrix products, arithmetic and copies ran while one was open for 7% -> 0% of each run, Pallas kernels for 0% -> 0%
where the time goes in v1:
time: 102 us
  Pallas kernels  98.5 us (97%)
  local copies, waits for them, and re-layouts  2.53 us (2%)
    pallas_call x1, Pallas kernels, local(): pl.pallas_call(kernel, out_shape=jax.ShapeDtypeStruct((8, T), F32), in_sp...  98.5 us

profile of v1, /device:TPU:1, one launch (start us, length us, event | category | flops | bytes accessed | tf_op | source)
XLA Modules:
  0.0 101.7 jit_solution(6761117983083368339)
XLA Ops:
  0.7 98.5 %heads.1 = f32[8,512]{1,0:T(8,128)} custom-call(bf16[1,8,7168]{2,1,0:T(8,128)(2,1)} %hid_ref.1, bf16[1010,7168]{1,0:T(8,128)(2,1)} %emb_ref.1, s32[1,8]{1,0:T(1,128)} %tgt_ref.1, s32[1,8]{1,0:T(1,128)} %mask_ref.1), custom_call_target="tpu_custom_call" | custom-call | tf_op jit(solution)/shard_map/heads/pallas_call | solution.py:433
  99.2 1.3 %constant_dynamic-slice_fusion = f32[1,8]{1,0:T(1,128)} fusion(f32[8,512]{1,0:T(8,128)} %heads.1, s32[]{:T(128)S(6)} %select_n.27), kind=kLoop, calls=%fused_computation | loop fusion | bytes 68 | tf_op jit(solution)/shard_map/dynamic_slice | solution.py:483
  100.4 1.3 %fusion = (f32[1,1]{1,0:T(1,128)}, f32[1,1]{1,0:T(1,128)}) fusion(f32[8,512]{1,0:T(8,128)} %heads.1), kind=kLoop, calls=%fused_computation.1 | loop fusion | bytes 16 | tf_op jit(solution)/shard_map/slice | solution.py:484

commit v2 on v1

v2 whole, which is shorter than its diff:
```python
import jax
import jax.numpy as jnp
from jax import lax
from jax.experimental import pallas as pl
from jax.experimental.pallas import tpu as pltpu
from jax.sharding import Mesh
from jax.sharding import PartitionSpec as P

MESH = pl.DeviceIdType.MESH
F32 = jnp.float32
BF16 = jnp.bfloat16

VOC = 1010
VPAD = 1024
D = 7168
T = 512
SLICES = 7
WIDTH = D // SLICES
SUBS = 4
SUBW = WIDTH // SUBS
STEPS = 4
LAG = 2
NEUTRAL = -1e30
SHIFT = 13.862943611198906
CYCLE = (5, 3, 4, 2)


def kernel(
    hid_ref, emb_ref, tgt_ref, mask_ref, nll_ref, loss_ref, norm_ref,
    hx, emb, l, b, xall, w, wp, ep, y, yx,
    ints1, ints2, st1, st2, fin1, fin2, live_buf, cols_buf,
    hid_sem, emb_sem, hs, hr, xs, xr, hps, hpr, es, er,
    is1, ir1, is2, ir2, ss1, sr1, ss2, sr2, fs1, fr1, fs2, fr2,
):
    ms, md, mz, my, mx = (lax.axis_index(a) for a in ("s", "d", "zl", "y", "x"))
    zz = md * 2 + mz
    qx1, qx0 = mx // 2, (mx + mx // 2) % 2
    qy1, qy0 = my // 2, (my + my // 2) % 2
    mine = (ms, mz, qy1, qy0, qx1, qx0)
    partner = {
        5: {"x": mx + 1 - 2 * (mx % 2)},
        4: {"x": 3 - mx},
        3: {"y": my + 1 - 2 * (my % 2)},
        2: {"y": 3 - my},
        1: {"zl": 1 - mz},
        0: {"s": 1 - ms},
    }
    item = ((((ms * 2 + mz) * 2 + qy1) * 2 + qy0) * 2 + qx1) * 2 + qx0
    col_id = ms * 4 + zz
    plane_id = my * 4 + mx
    h2 = hx.at[pl.ds(0, T)]
    h = h2.reshape(2, 2, 2, 2, 2, 2, 8, D)
    partner_rows = hx.at[pl.ds(T, 8)]
    x2 = xall.reshape(T, T)

    def col_peer(k):
        z = (zz + k % 4) % 4
        return {"s": (ms + k // 4) % 2, "d": z // 2, "zl": z % 2}

    def plane_peer(k):
        return {"y": (my + k // 4) % 4, "x": (mx + k % 4) % 4}

    def zx_peer(k):
        return {"zl": (mz + k // 4) % 2, "x": (mx + k % 4) % 4}

    def zy_peer(k):
        return {"zl": (mz + k // 4) % 2, "y": (my + k % 4) % 4}

    def wait_bytes(ref, sem):
        pltpu.make_async_copy(ref, ref, sem).wait()

    def send(src, dst, ssem, rsem, dev):
        pltpu.make_async_remote_copy(
            src_ref=src, dst_ref=dst, send_sem=ssem, recv_sem=rsem,
            device_id=dev, device_id_type=MESH).start()

    own = pltpu.make_async_copy(hid_ref.at[0], h.at[mine], hid_sem)
    own.start()

    def emb_copy(c):
        cs = pl.ds(pl.multiple_of(c * WIDTH, WIDTH), WIDTH)
        return pltpu.make_async_copy(emb_ref.at[:, cs], emb.at[:, cs], emb_sem.at[c])

    barrier = pltpu.get_barrier_semaphore()
    greeted = [col_peer(k) for k in range(1, 8)] + [plane_peer(k) for k in range(1, 16)]
    greeted += [zx_peer(k) for k in range(5, 8)] + [zy_peer(k) for k in range(5, 8)]
    for dev in greeted:
        pl.semaphore_signal(barrier, inc=1, device_id=dev, device_id_type=MESH)
    for c in range(SLICES):
        emb_copy(c).start()

    lane = lax.broadcasted_iota(jnp.int32, (8, T), 1)
    row8 = lax.broadcasted_iota(jnp.int32, (8, T), 0)
    ints = jnp.zeros((8, T), jnp.int32)
    for i in range(8):
        here = lane == item * 8 + i
        ints = jnp.where(here & (row8 == md), tgt_ref[0, i], ints)
        ints = jnp.where(here & (row8 == 2 + md), mask_ref[0, i], ints)
    ints1[col_id] = ints
    l[...] = jnp.zeros_like(l)
    b[...] = jnp.zeros_like(b)
    own.wait()
    pl.semaphore_wait(barrier, len(greeted))

    def share(buf, my_slot, peer, count, ssem, rsem):
        for k in range(1, count):
            send(buf.at[my_slot], buf.at[my_slot], ssem, rsem, peer(k))

    def box(held, cs):
        return tuple(slice(None) if dim in held else mine[dim] for dim in range(6)) + (slice(None), cs)

    def columns(start, width):
        return pl.ds(pl.multiple_of(start, width), width)

    def cube_send(c, step):
        for sub in range(SUBS):
            dims = [CYCLE[(sub + k) % 4] for k in range(4)]
            where = h.at[box((1, *dims[:step]), columns(c * WIDTH + sub * SUBW, SUBW))]
            send(where, where, hs, hr.at[c, 1 + step], partner[dims[step]])

    def cube_wait(c, step):
        wait_bytes(h2.at[pl.ds(0, 16 * 2**step), columns(c * WIDTH, WIDTH)], hr.at[c, 1 + step])

    for c in range(SLICES):
        where = h.at[(*mine, slice(None), columns(c * WIDTH, WIDTH))]
        send(where, where, hs, hr.at[c, 0], partner[1])
    send(h.at[mine], partner_rows, hps, hpr, {"d": 1 - md})
    share(ints1, col_id, col_peer, 8, is1, ir1)

    def nt(lhs, rhs):
        return lax.dot_general(lhs, rhs, (((1,), (1,)), ((), ())), preferred_element_type=F32)

    def body(i, carry):
        c4 = i - 4 * LAG

        @pl.when((c4 >= 0) & (c4 < SLICES))
        def _():
            cube_wait(c4, 3)
            where = h.at[box((1, 2, 3, 4, 5), columns(c4 * WIDTH, WIDTH))]
            send(where, where, hs, hr.at[c4, 5], partner[0])

        for step in (3, 2, 1):
            c = i - step * LAG

            @pl.when((c >= 0) & (c < SLICES))
            def _(c=c, step=step):
                cube_wait(c, step - 1)
                cube_send(c, step)

        @pl.when(i < SLICES)
        def _():
            wait_bytes(h2.at[pl.ds(0, 8), columns(i * WIDTH, WIDTH)], hr.at[i, 0])
            cube_send(i, 0)

        @pl.when(i == 4)
        def _():
            wait_bytes(partner_rows, hpr)
            wait_bytes(ints1.at[pl.ds(0, 7)], ir1)
            ints2[plane_id] = sum(ints1[k] for k in range(8))
            share(ints2, plane_id, plane_peer, 16, is2, ir2)

        c5 = i - 4 * LAG - 1

        @pl.when(c5 >= 0)
        def _():
            wait_bytes(h2.at[pl.ds(0, 256), columns(c5 * WIDTH, WIDTH)], hr.at[c5, 5])
            emb_copy(c5).wait()
            cs = columns(c5 * WIDTH, WIDTH)

            def half(n, carry):
                ts = pl.ds(pl.multiple_of(n * 256, 256), 256)
                hn = h2[ts, cs]
                l[0:VOC, ts] += nt(emb[:, cs], hn)
                b[:, ts] += nt(hx[:, cs], hn)
                return carry

            lax.fori_loop(0, 2, half, 0)

        return carry

    lax.fori_loop(0, SLICES + 4 * LAG + 1, body, 0)

    xall[mine] = b[T : T + 8]
    left, right = pl.ds(0, T // 2), pl.ds(T // 2, T // 2)
    for k in range(1, 8):
        for cs, sem, peer in ((left, 0, zx_peer), (right, 1, zy_peer)):
            where = xall.at[(*mine, slice(None), cs)]
            send(where, where, xs, xr.at[sem], peer(k))

    wait_bytes(ints2.at[pl.ds(0, 15)], ir2)
    ints = sum(ints2[k] for k in range(16))
    first_id = (ms * 32 + mz * 16 + my * 4 + mx) * VOC
    local_t = ints[0:2] - first_id
    local_t = jnp.where(local_t < VOC, local_t, -1)
    own_t = jnp.where(md == 0, local_t[0:1], local_t[1:2])
    other_t = jnp.where(md == 0, local_t[1:2], local_t[0:1])
    live_buf[0:2] = ints[2:4].astype(F32)

    tail = l[VOC - 2 : VPAD]
    tail_row = lax.broadcasted_iota(jnp.int32, tail.shape, 0)
    l[VOC - 2 : VPAD] = jnp.where(tail_row < 2, tail, NEUTRAL)
    blk = 64
    groups = blk // 8
    rows = lax.broadcasted_iota(jnp.int32, (blk, T), 0)

    def peak_body(i, carry):
        peak, chosen = carry
        at = pl.multiple_of(i * blk, blk)
        part = l[pl.ds(at, blk)]
        hit = (rows + at) == own_t
        peak = jnp.maximum(peak, jnp.max(part.reshape(groups, 8, T), axis=0))
        chosen = chosen + jnp.sum(jnp.where(hit, part, 0.0).reshape(groups, 8, T), axis=0)
        return peak, chosen

    peak, chosen = lax.fori_loop(
        0, VPAD // blk, peak_body,
        (jnp.full((8, T), NEUTRAL, F32), jnp.zeros((8, T), F32)))
    origin = jnp.max(peak, axis=0, keepdims=True) - SHIFT
    chosen = jnp.sum(chosen, axis=0, keepdims=True)

    def exp_body(i, total):
        at = pl.multiple_of(i * blk, blk)
        e = jnp.exp(l[pl.ds(at, blk)] - origin)
        hit = (rows + at) == own_t
        w[pl.ds(at, blk), 0:T] = jnp.where(hit, 0.0, e).astype(BF16)
        w[pl.ds(at, blk), T : 2 * T] = jnp.where(hit, 1.0, 0.0).astype(BF16)
        return total + jnp.sum(e.reshape(groups, 8, T), axis=0)

    total = lax.fori_loop(0, VPAD // blk, exp_body, jnp.zeros((8, T), F32))
    total = jnp.sum(total, axis=0, keepdims=True)
    stats = jnp.where(row8 < 2, NEUTRAL, jnp.zeros((8, T), F32))
    stats = jnp.where(row8 == md, origin, stats)
    stats = jnp.where(row8 == 2 + md, total, stats)
    stats = jnp.where(row8 == 4 + md, chosen, stats)
    st1[col_id] = stats
    share(st1, col_id, col_peer, 8, ss1, sr1)

    half_rows = VPAD // 2
    theirs = pl.ds(pl.multiple_of((1 - md) * half_rows, half_rows), half_rows)
    ours = pl.ds(pl.multiple_of(md * half_rows, half_rows), half_rows)
    send(w.at[theirs, pl.ds(0, T)], ep, es, er, {"d": 1 - md})

    gb = 256

    def gram_own(i, carry):
        at = pl.multiple_of(i * gb, gb)
        brow = pl.multiple_of((i % (T // gb)) * gb, gb)
        lhs = w[:, pl.ds(at, gb)]
        bb = b[pl.ds(brow, gb), :]
        for n in range(2):
            part = lax.dot_general(
                lhs, w[:, n * T : (n + 1) * T], (((0,), (0,)), ((), ())),
                preferred_element_type=F32)
            y[pl.ds(at, gb), n * T : (n + 1) * T] = part * bb
        return carry

    lax.fori_loop(0, 2 * T // gb, gram_own, 0)

    def merge(parts):
        top = parts[0][0:2]
        for p in parts[1:]:
            top = jnp.maximum(top, p[0:2])
        tot = jnp.zeros((2, T), F32)
        pick = jnp.zeros((2, T), F32)
        for p in parts:
            tot = tot + p[2:4] * jnp.exp(p[0:2] - top)
            pick = pick + p[4:6]
        return top, tot, pick

    wait_bytes(st1.at[pl.ds(0, 7)], sr1)
    top, tot, pick = merge([st1[k] for k in range(8)])
    st2[plane_id, 0:2] = top
    st2[plane_id, 2:4] = tot
    st2[plane_id, 4:6] = pick
    st2[plane_id, 6:8] = jnp.zeros((2, T), F32)
    share(st2, plane_id, plane_peer, 16, ss2, sr2)

    wait_bytes(x2.at[pl.ds(0, 56), left], xr.at[0])
    wait_bytes(x2.at[pl.ds(0, 56), right], xr.at[1])
    for k in range(1, 4):
        for cs, sem, held, peer in ((left, 2, (1, 4, 5), {"y": (my + k) % 4}), (right, 3, (1, 2, 3), {"x": (mx + k) % 4})):
            where = xall.at[box(held, cs)]
            send(where, where, xs, xr.at[sem], peer)

    def other_hot(i, carry):
        at = pl.multiple_of(i * blk, blk)
        hit = (rows + (at + md * half_rows)) == other_t
        wp[pl.ds(at, blk), T : 2 * T] = jnp.where(hit, 1.0, 0.0).astype(BF16)
        return carry

    lax.fori_loop(0, half_rows // blk, other_hot, 0)

    wait_bytes(x2.at[pl.ds(0, 192), left], xr.at[2])
    wait_bytes(x2.at[pl.ds(0, 192), right], xr.at[3])
    where = xall.at[ms]
    send(where, where, xs, xr.at[4], partner[0])

    wait_bytes(st2.at[pl.ds(0, 15)], sr2)
    top, tot, pick = merge([st2[k] for k in range(16)])
    lse = top + jnp.log(tot)
    nll = lse - pick
    live = live_buf[0:2]
    weight = jnp.where(lax.broadcasted_iota(jnp.int32, (2, 1), 0) == 0, 1.0, 0.3).astype(F32)
    coef = weight / jnp.maximum(jnp.sum(live, axis=1, keepdims=True), 1.0)
    loss = jnp.sum(coef * jnp.sum(live * nll, axis=1, keepdims=True), axis=0, keepdims=True)
    scale = coef * live
    g = (scale * (jnp.exp(pick - lse) - 1.0)).astype(BF16).astype(F32)
    partner_slot = ms * 4 + (1 - md) * 2 + mz
    origin_p = jnp.where(md == 0, st1[partner_slot, 1:2], st1[partner_slot, 0:1])

    def pair(a):
        return (jnp.where(md == 0, a[0:1], a[1:2]), jnp.where(md == 0, a[1:2], a[0:1]))

    scale_o, scale_p = pair(scale)
    lse_o, lse_p = pair(lse)
    g_o, g_p = pair(g)
    s_o = scale_o * jnp.exp(origin - lse_o)
    s_p = scale_p * jnp.exp(origin_p - lse_p)
    vecs = jnp.where(row8 == 0, s_o, jnp.where(row8 == 1, g_o, jnp.where(row8 == 2, s_p, jnp.where(row8 == 3, g_p, 0.0))))
    cols_buf[...] = vecs.T

    wait_bytes(ep, er)
    wp[:, 0:T] = ep[...]
    wait_bytes(xall.at[ms], xr.at[4])

    def gram_cross(i, carry):
        at = pl.multiple_of(i * gb, gb)
        brow = pl.multiple_of((i % (T // gb)) * gb, gb)
        lhs = wp[:, pl.ds(at, gb)]
        bb = x2[pl.ds(brow, gb), :]
        for n in range(2):
            part = lax.dot_general(
                lhs, w[ours, n * T : (n + 1) * T], (((0,), (0,)), ((), ())),
                preferred_element_type=F32)
            yx[pl.ds(at, gb), n * T : (n + 1) * T] = part * bb
        return carry

    lax.fori_loop(0, 2 * T // gb, gram_cross, 0)

    qb = 64

    def quad(i, carry):
        acc_s, acc_g = carry
        at = pl.multiple_of(i * qb, qb)
        cols = cols_buf[pl.ds(at, qb), :]
        at2 = pl.multiple_of(T + at, qb)
        so, go, sp, gp = (cols[:, k : k + 1] for k in range(4))
        sp, gp = 2.0 * sp, 2.0 * gp
        lhs = (so * y[pl.ds(at, qb), 0:T] + go * y[pl.ds(at2, qb), 0:T]
               + sp * yx[pl.ds(at, qb), 0:T] + gp * yx[pl.ds(at2, qb), 0:T])
        rhs = (so * y[pl.ds(at, qb), T : 2 * T] + go * y[pl.ds(at2, qb), T : 2 * T]
               + sp * yx[pl.ds(at, qb), T : 2 * T] + gp * yx[pl.ds(at2, qb), T : 2 * T])
        acc_s = acc_s + jnp.sum(lhs.reshape(qb // 8, 8, T), axis=0)
        acc_g = acc_g + jnp.sum(rhs.reshape(qb // 8, 8, T), axis=0)
        return acc_s, acc_g

    zero = jnp.zeros((8, T), F32)
    acc_s, acc_g = lax.fori_loop(0, T // qb, quad, (zero, zero))
    q = jnp.sum(jnp.sum(acc_s * s_o + acc_g * g_o, axis=0, keepdims=True), axis=1, keepdims=True)
    fin1[col_id] = jnp.broadcast_to(q, (8, 128))
    share(fin1, col_id, col_peer, 8, fs1, fr1)

    wait_bytes(h2.at[pl.ds(0, T - 8)], hs)
    wait_bytes(x2.at[pl.ds(0, T - 8)], xs)
    wait_bytes(partner_rows, hps)
    wait_bytes(ep, es)
    wait_bytes(ints1.at[pl.ds(0, 7)], is1)
    wait_bytes(ints2.at[pl.ds(0, 15)], is2)
    wait_bytes(st1.at[pl.ds(0, 7)], ss1)
    wait_bytes(st2.at[pl.ds(0, 15)], ss2)
    nll_own, _ = pair(nll)
    turned = pltpu.roll(jnp.broadcast_to(nll_own, (8, T)), (T - item * 8) % T, 1)
    nll_ref[...] = turned[0:1, 0:8]
    loss_ref[...] = loss

    wait_bytes(fin1.at[pl.ds(0, 7)], fr1)
    fin2[plane_id] = sum(fin1[k] for k in range(8))
    share(fin2, plane_id, plane_peer, 16, fs2, fr2)
    wait_bytes(fin1.at[pl.ds(0, 7)], fs1)
    wait_bytes(fin2.at[pl.ds(0, 15)], fr2)
    norm = jnp.sqrt(jnp.maximum(sum(fin2[k] for k in range(16)), 0.0))
    norm_ref[...] = norm[0:1, 0:1]
    wait_bytes(fin2.at[pl.ds(0, 15)], fs2)


def local(hidden, embedding, targets, mask):
    dma = pltpu.SemaphoreType.DMA
    vmem, smem = pl.BlockSpec(memory_space=pltpu.VMEM), pl.BlockSpec(memory_space=pltpu.SMEM)
    whole = pl.BlockSpec(memory_space=pl.ANY)
    nll, loss, norm = pl.pallas_call(
        kernel,
        out_shape=(
            jax.ShapeDtypeStruct((1, 8), F32),
            jax.ShapeDtypeStruct((1, 1), F32),
            jax.ShapeDtypeStruct((1, 1), F32),
        ),
        in_specs=[whole, whole, smem, smem],
        out_specs=(vmem, vmem, vmem),
        scratch_shapes=[
            pltpu.VMEM((T + 8, D), BF16),
            pltpu.VMEM((VOC, D), BF16),
            pltpu.VMEM((VPAD, T), F32),
            pltpu.VMEM((T + 8, T), F32),
            pltpu.VMEM((2, 2, 2, 2, 2, 2, 8, T), F32),
            pltpu.VMEM((VPAD, 2 * T), BF16),
            pltpu.VMEM((VPAD // 2, 2 * T), BF16),
            pltpu.VMEM((VPAD // 2, T), BF16),
            pltpu.VMEM((2 * T, 2 * T), F32),
            pltpu.VMEM((2 * T, 2 * T), F32),
            pltpu.VMEM((8, 8, T), jnp.int32),
            pltpu.VMEM((16, 8, T), jnp.int32),
            pltpu.VMEM((8, 8, T), F32),
            pltpu.VMEM((16, 8, T), F32),
            pltpu.VMEM((8, 8, 128), F32),
            pltpu.VMEM((16, 8, 128), F32),
            pltpu.VMEM((8, T), F32),
            pltpu.VMEM((T, 8), F32),
            dma,
            dma((SLICES,)),
            dma,
            dma((SLICES, 6)),
            dma,
            dma((5,)),
            dma, dma, dma, dma,
            dma, dma, dma, dma,
            dma, dma, dma, dma,
            dma, dma, dma, dma,
        ],
        compiler_params=pltpu.CompilerParams(collective_id=0, has_side_effects=True),
        name="heads",
    )(hidden, embedding, targets, mask)
    return (nll, loss[0, 0], norm[0, 0])


def solution(mesh):
    torus = Mesh(mesh.devices.reshape(2, 2, 2, 4, 4), ("s", "d", "zl", "y", "x"))
    group = ("s", "zl", "y", "x")
    return jax.shard_map(
        local,
        mesh=torus,
        in_specs=(P("d", group, None), P(group, None), P("d", group), P("d", group)),
        out_specs=(P("d", group), P(), P()),
        check_vma=False,
    )
```

time: 102 us -> 81.8 us (0.80)
  Pallas kernels: 98.5 us -> 76.3 us
  between operations: 0.71 us -> 4.16 us
  local copies, waits for them, and re-layouts: 2.53 us -> 1.11 us
    pallas_call x1, Pallas kernels: 98.5 us -> 76.3 us  [local(): pl.pallas_call(kernel, out_shape=(jax.ShapeDtypeStruct((1, 8), F32), jax....]
    dynamic_slice x1 -> x0, local copies, waits for them, and re-layouts: 1.27 us -> none  [local(): nll = lax.dynamic_slice(out, (0, item * 8), (1, 8))]
    slice x1 -> x0, local copies, waits for them, and re-layouts: 1.26 us -> none  [local(): return (nll, out[1, 0], out[2, 0])]
    unnamed x0 -> x1, local copies, waits for them, and re-layouts: none -> 1.11 us
where the time goes in v2:
time: 81.8 us; the launch traced here: 81.6 us
  Pallas kernels  76.3 us (93%)
  between operations  4.16 us (5%)
  local copies, waits for them, and re-layouts  1.11 us (1%)
    pallas_call x1, Pallas kernels, local(): pl.pallas_call(kernel, out_shape=(jax.ShapeDtypeStruct((1, 8), F32), jax....  76.3 us

profile of v2, /device:TPU:1, one launch (start us, length us, event | category | flops | bytes accessed | tf_op | source)
XLA Modules:
  0.0 81.6 jit_solution(16114332001963253519)
XLA Ops:
  0.6 76.3 %heads.1 = (f32[1,8]{1,0:T(1,128)}, f32[1,1]{1,0:T(1,128)}, f32[1,1]{1,0:T(1,128)}) custom-call(bf16[1,8,7168]{2,1,0:T(8,128)(2,1)} %hid_ref.1, bf16[1010,7168]{1,0:T(8,128)(2,1)} %emb_ref.1, s32[1,8]{1,0:T(1,128)} %tgt_ref.1, s32[1,8]{1,0:T(1,128)} %mask_ref.1), custom_call_target="tpu_custom_call" | custom-call | tf_op jit(solution)/shard_map/heads/pallas_call | solution.py:390
  77.0 1.1 %copy.10 = f32[1,8]{1,0:T(1,128)} copy(f32[1,8]{1,0:T(1,128)} %get-tuple-element.12) | data formatting | bytes 64

commit v3 on v2

v3 whole, which is shorter than its diff:
```python
import jax
import jax.numpy as jnp
from jax import lax
from jax.experimental import pallas as pl
from jax.experimental.pallas import tpu as pltpu
from jax.sharding import Mesh
from jax.sharding import PartitionSpec as P

MESH = pl.DeviceIdType.MESH
F32 = jnp.float32
BF16 = jnp.bfloat16

VOC = 1010
VPAD = 1024
D = 7168
T = 512
SLICES = 7
WIDTH = D // SLICES
HALF = T // 2
SUBS = 4
SUBW = WIDTH // SUBS
LEAD = 2
LAG = 2
FIRST = SLICES + LEAD - 4 * LAG
TURN_A = SLICES + LEAD
NEUTRAL = -1e30
SHIFT = 13.862943611198906
CYCLE = (5, 3, 4, 2)


def kernel(
    hid_ref, emb_ref, tgt_ref, mask_ref, out_ref,
    hx, emb, l, b, xt, xall, w, wp, ep, y, yo, yx,
    ints1, ints2, st1, st2, fin1, fin2, live_buf, tgt_buf, orig_buf, tcols_buf, cols_buf,
    hid_sem, emb_sem, hs, hr, xs, xr, hps, hpr, es, er,
    is1, ir1, is2, ir2, ss1, sr1, ss2, sr2, fs1, fr1, fs2, fr2,
):
    ms, md, mz, my, mx = (lax.axis_index(a) for a in ("s", "d", "zl", "y", "x"))
    zz = md * 2 + mz
    qx1, qx0 = mx // 2, (mx + mx // 2) % 2
    qy1, qy0 = my // 2, (my + my // 2) % 2
    mine = (mz, ms, qy1, qy0, qx1, qx0)
    partner = {
        5: {"x": mx + 1 - 2 * (mx % 2)},
        4: {"x": 3 - mx},
        3: {"y": my + 1 - 2 * (my % 2)},
        2: {"y": 3 - my},
    }
    core, other_plane = {"s": 1 - ms}, {"zl": 1 - mz}
    item = ((((mz * 2 + ms) * 2 + qy1) * 2 + qy0) * 2 + qx1) * 2 + qx0
    col_id = ms * 4 + zz
    plane_id = my * 4 + mx
    h2 = hx.at[pl.ds(0, T)]
    h = h2.reshape(2, 2, 2, 2, 2, 2, 8, D)
    partner_rows = hx.at[pl.ds(T, 8)]
    x2 = xall.reshape(T, T)

    def col_peer(k):
        z = (zz + k % 4) % 4
        return {"s": (ms + k // 4) % 2, "d": z // 2, "zl": z % 2}

    def plane_peer(k):
        return {"y": (my + k // 4) % 4, "x": (mx + k % 4) % 4}

    def zx_peer(k):
        return {"zl": (mz + k // 4) % 2, "x": (mx + k % 4) % 4}

    def zy_peer(k):
        return {"zl": (mz + k // 4) % 2, "y": (my + k % 4) % 4}

    def wait_bytes(ref, sem):
        pltpu.make_async_copy(ref, ref, sem).wait()

    def send(src, dst, ssem, rsem, dev):
        pltpu.make_async_remote_copy(
            src_ref=src, dst_ref=dst, send_sem=ssem, recv_sem=rsem,
            device_id=dev, device_id_type=MESH).start()

    own = pltpu.make_async_copy(hid_ref.at[0], h.at[mine], hid_sem)
    own.start()

    def emb_copy(c):
        cs = pl.ds(pl.multiple_of(c * WIDTH, WIDTH), WIDTH)
        return pltpu.make_async_copy(emb_ref.at[:, cs], emb.at[:, cs], emb_sem.at[c])

    barrier = pltpu.get_barrier_semaphore()
    greeted = [col_peer(k) for k in range(1, 8)] + [plane_peer(k) for k in range(1, 16)]
    greeted += [zx_peer(k) for k in range(5, 8)] + [zy_peer(k) for k in range(5, 8)]
    for dev in greeted:
        pl.semaphore_signal(barrier, inc=1, device_id=dev, device_id_type=MESH)
    for c in range(SLICES):
        emb_copy(c).start()

    lane = lax.broadcasted_iota(jnp.int32, (8, T), 1)
    row8 = lax.broadcasted_iota(jnp.int32, (8, T), 0)
    ints = jnp.zeros((8, T), jnp.int32)
    for i in range(8):
        here = lane == item * 8 + i
        ints = jnp.where(here & (row8 == md), tgt_ref[0, i], ints)
        ints = jnp.where(here & (row8 == 2 + md), mask_ref[0, i], ints)
    ints1[col_id] = ints
    l[...] = jnp.zeros_like(l)
    b[...] = jnp.zeros_like(b)
    xt[...] = jnp.zeros_like(xt)
    own.wait()
    pl.semaphore_wait(barrier, len(greeted))

    def share(buf, my_slot, peer, count, ssem, rsem):
        for k in range(1, count):
            send(buf.at[my_slot], buf.at[my_slot], ssem, rsem, peer(k))

    def box(held, cs, plane=mz):
        at = (plane, *mine[1:])
        return tuple(slice(None) if dim in held else at[dim] for dim in range(6)) + (slice(None), cs)

    def columns(start, width):
        return pl.ds(pl.multiple_of(start, width), width)

    def slice_wait(unit, c, stage, items):
        wait_bytes(h2.at[pl.ds(0, 8 * items), columns(c * WIDTH, WIDTH)], hr.at[unit, stage])

    def x_peer(k):
        return {"x": (mx + k) % 4}

    def y_peer(k):
        return {"y": (my + k) % 4}

    def direct_send(c, stage):
        for sub, (first, second, held) in enumerate(((x_peer, y_peer, (4, 5)), (y_peer, x_peer, (2, 3)))):
            cs = columns(c * WIDTH + sub * (WIDTH // 2), WIDTH // 2)
            where = h.at[box(held if stage else (), cs)]
            for k in (2, 1, 3):
                send(where, where, hs, hr.at[c, stage], (second if stage else first)(k))

    def cube_send(c, step):
        for sub in range(SUBS):
            dims = [CYCLE[(sub + k) % 4] for k in range(4)]
            where = h.at[box(dims[:step], columns(c * WIDTH + sub * SUBW, SUBW), 1 - mz)]
            send(where, where, hs, hr.at[SLICES + c, 1 + step], partner[dims[step]])

    def core_send(unit, c, plane, stage):
        where = h.at[box((2, 3, 4, 5), columns(c * WIDTH, WIDTH), plane)]
        send(where, where, hs, hr.at[unit, stage], core)

    for c in range(SLICES):
        direct_send(c, 0)
    send(h.at[mine], partner_rows, hps, hpr, {"d": 1 - md})
    for c in range(SLICES):
        where = h.at[(*mine, slice(None), columns(c * WIDTH, WIDTH))]
        send(where, where, hs, hr.at[SLICES + c, 0], other_plane)
    share(ints1, col_id, col_peer, 8, is1, ir1)

    def nt(lhs, rhs):
        return lax.dot_general(lhs, rhs, (((1,), (1,)), ((), ())), preferred_element_type=F32)

    blk = 128
    groups = blk // 8
    rows = lax.broadcasted_iota(jnp.int32, (blk, HALF), 0)
    half_rows = VPAD // 2
    theirs = pl.ds(pl.multiple_of((1 - md) * half_rows, half_rows), half_rows)
    ours = pl.ds(pl.multiple_of(md * half_rows, half_rows), half_rows)

    def cross_columns(n):
        return tuple(columns(n * HALF + k * (HALF // 2), HALF // 2) for k in range(2))

    def cross_first(n, phase):
        xall[(*mine, slice(None), columns(n * HALF, HALF))] = xt[columns(n * HALF, HALF), :].T
        for k in range(1, 8):
            for sub, (cs, peer) in enumerate(zip(cross_columns(n), (zx_peer, zy_peer))):
                where = xall.at[(*mine, slice(None), cs)]
                send(where, where, xs, xr.at[phase, sub], peer(k))

    def cross_second(phase):
        for sub in range(2):
            wait_bytes(x2.at[pl.ds(0, 56), pl.ds(0, HALF // 2)], xr.at[phase, sub])
        for plane in range(2):
            halves = cross_columns(plane ^ phase)
            for k in (2, 1, 3):
                for sub, (cs, held, peer) in enumerate(zip(halves, ((4, 5), (2, 3)), (y_peer, x_peer))):
                    where = xall.at[box(held, cs, plane)]
                    send(where, where, xs, xr.at[phase, 2 + sub], peer(k))

    def cross_third(phase):
        for sub in range(2):
            wait_bytes(x2.at[pl.ds(0, 192), pl.ds(0, HALF // 2)], xr.at[phase, 2 + sub])
        for plane in range(2):
            where = xall.at[plane, ms, :, :, :, :, :, columns((plane ^ phase) * HALF, HALF)]
            send(where, where, xs, xr.at[phase, 4], core)

    def cross_wait(phase):
        wait_bytes(x2.at[pl.ds(0, 256), pl.ds(0, HALF)], xr.at[phase, 4])

    def finish_half(n, phase):
        ls = columns(n * HALF, HALF)
        cross_first(n, phase)
        own_t = tgt_buf[0:1, ls]

        def peak_body(i, carry):
            peak, chosen = carry
            at = pl.multiple_of(i * blk, blk)
            part = l[pl.ds(at, blk), ls]
            hit = (rows + at) == own_t
            peak = jnp.maximum(peak, jnp.max(part.reshape(groups, 8, HALF), axis=0))
            chosen = chosen + jnp.sum(jnp.where(hit, part, 0.0).reshape(groups, 8, HALF), axis=0)
            return peak, chosen

        peak, chosen = lax.fori_loop(
            0, VPAD // blk, peak_body,
            (jnp.full((8, HALF), NEUTRAL, F32), jnp.zeros((8, HALF), F32)))
        origin = jnp.max(peak, axis=0, keepdims=True) - SHIFT
        chosen = jnp.sum(chosen, axis=0, keepdims=True)

        def exp_body(i, total):
            at = pl.multiple_of(i * blk, blk)
            e = jnp.exp(l[pl.ds(at, blk), ls] - origin)
            hit = (rows + at) == own_t
            w[pl.ds(at, blk), ls] = jnp.where(hit, 0.0, e).astype(BF16)
            w[pl.ds(at, blk), columns(T + n * HALF, HALF)] = jnp.where(hit, 1.0, 0.0).astype(BF16)
            return total + jnp.sum(e.reshape(groups, 8, HALF), axis=0)

        total = lax.fori_loop(0, VPAD // blk, exp_body, jnp.zeros((8, HALF), F32))
        total = jnp.sum(total, axis=0, keepdims=True)
        st1[phase, plane_id] = tile(origin, total, chosen)
        orig_buf[0:1, ls] = origin
        share(st1.at[phase], plane_id, plane_peer, 16, ss1, sr1.at[phase])

    def tile(*lines):
        out = jnp.zeros((8, 128), F32)
        for k, line in enumerate(lines):
            for part in range(2):
                out = jnp.where(row8[:, 0:128] == 2 * k + part, line[:, part * 128 : (part + 1) * 128], out)
        return out

    def merge(parts):
        top = parts[0][0:2]
        for p in parts[1:]:
            top = jnp.maximum(top, p[0:2])
        tot = jnp.zeros((2, 128), F32)
        pick = jnp.zeros((2, 128), F32)
        for p in parts:
            tot = tot + p[2:4] * jnp.exp(p[0:2] - top)
            pick = pick + p[4:6]
        return top, tot, pick

    def plane_merge(n, phase):
        wait_bytes(st1.at[phase, pl.ds(0, 15)], sr1.at[phase])
        top, tot, pick = merge([st1[phase, k] for k in range(16)])
        st2[col_id, n, 0:2] = top
        st2[col_id, n, 2:4] = tot
        st2[col_id, n, 4:6] = pick
        own_origin = orig_buf[0:1, columns(n * HALF, HALF)]
        st2[col_id, n, 6:7] = own_origin[:, 0:128]
        st2[col_id, n, 7:8] = own_origin[:, 128:256]

    def exchange(n, phase):
        ls = columns(n * HALF, HALF)
        send(w.at[theirs, ls], ep.at[:, ls], es, er.at[phase], {"d": 1 - md})

    def body(i, carry):
        @pl.when(i < SLICES)
        def _():
            slice_wait(i, i, 0, 3)
            direct_send(i, 1)

        c = i - LEAD

        @pl.when((c >= 0) & (c < SLICES))
        def _():
            slice_wait(c, c, 1, 12)
            core_send(c, c, mz, 2)

        c4 = i - FIRST - 4 * LAG

        @pl.when((c4 >= 0) & (c4 < SLICES))
        def _():
            slice_wait(SLICES + c4, c4, 4, 8)
            core_send(SLICES + c4, c4, 1 - mz, 5)

        for step in (3, 2, 1, 0):
            c = i - FIRST - step * LAG

            @pl.when((c >= 0) & (c < SLICES))
            def _(c=c, step=step):
                slice_wait(SLICES + c, c, step, 2 ** max(step - 1, 0))
                cube_send(c, step)

        @pl.when(i == 5)
        def _():
            wait_bytes(ints1.at[pl.ds(0, 7)], ir1)
            ints2[plane_id] = sum(ints1[k] for k in range(8))
            share(ints2, plane_id, plane_peer, 16, is2, ir2)

        u = i - LEAD - 1

        @pl.when(u == 0)
        def _():
            wait_bytes(partner_rows, hpr)

        @pl.when(u >= 0)
        def _():
            phase = u // SLICES
            c = u - phase * SLICES
            n = mz + phase * (1 - 2 * mz)

            @pl.when(phase == 0)
            def _():
                slice_wait(c, c, 2, 16)
                emb_copy(c).wait()

            @pl.when(phase == 1)
            def _():
                slice_wait(SLICES + c, c, 5, 16)

            cs, ls = columns(c * WIDTH, WIDTH), columns(n * HALF, HALF)
            hn = h2[ls, cs]
            l[0:VOC, ls] += nt(emb[:, cs], hn)
            xt[ls, :] += nt(hn, partner_rows[:, cs])

            @pl.when(phase == 0)
            def _():
                b[ls, ls] += nt(hn, hn)


        @pl.when(i == TURN_A)
        def _():
            wait_bytes(ints2.at[pl.ds(0, 15)], ir2)
            ints = sum(ints2[k] for k in range(16))
            first_id = (ms * 32 + mz * 16 + my * 4 + mx) * VOC
            local_t = ints[0:2] - first_id
            local_t = jnp.where(local_t < VOC, local_t, -1)
            tgt_buf[0:1] = jnp.where(md == 0, local_t[0:1], local_t[1:2])
            tgt_buf[1:2] = jnp.where(md == 0, local_t[1:2], local_t[0:1])
            live_buf[0:2] = ints[2:4].astype(F32)
            tail = l[VOC - 2 : VPAD]
            tail_row = lax.broadcasted_iota(jnp.int32, tail.shape, 0)
            l[VOC - 2 : VPAD] = jnp.where(tail_row < 2, tail, NEUTRAL)
            finish_half(mz, 0)
            exchange(mz, 0)

        @pl.when(i == TURN_A + 3)
        def _():
            cross_second(0)

        @pl.when(i == TURN_A + 5)
        def _():
            plane_merge(mz, 0)

        @pl.when(i == TURN_A + 6)
        def _():
            cross_third(0)

        return carry

    lax.fori_loop(0, 2 * SLICES + LEAD + 1, body, 0)

    finish_half(1 - mz, 1)
    exchange(1 - mz, 1)

    own_cols, late_cols = columns(mz * HALF, HALF), columns((1 - mz) * HALF, HALF)

    def late_b(c, carry):
        cs = columns(c * WIDTH, WIDTH)
        b[:, late_cols] += nt(h2[:, cs], h2[late_cols, cs])
        return carry

    lax.fori_loop(0, SLICES, late_b, 0)
    cross_second(1)
    b[late_cols, own_cols] = b[own_cols, late_cols].T

    tgt_rows = jnp.where(row8 < 2, jnp.broadcast_to(tgt_buf[0:1], (8, T)), 0).astype(F32)
    tcols_buf[...] = tgt_rows.T

    def tn(lhs, rhs):
        return lax.dot_general(lhs, rhs, (((0,), (0,)), ((), ())), preferred_element_type=F32)

    def gram_own(i, carry):
        rs = columns(i * HALF, HALF)
        lhs = w[:, rs]
        bb = b[rs, :]
        y[rs, 0:T] = tn(lhs, w[:, 0:T]) * bb
        y[rs, T : 2 * T] = tn(lhs, w[:, T : 2 * T]) * (2.0 * bb)
        return carry

    lax.fori_loop(0, 2, gram_own, 0)

    other_t = tgt_buf[1:2]
    rows_full = lax.broadcasted_iota(jnp.int32, (blk, T), 0)

    def other_hot(i, carry):
        at = pl.multiple_of(i * blk, blk)
        hit = (rows_full + (at + md * half_rows)) == other_t
        wp[pl.ds(at, blk), :] = jnp.where(hit, 1.0, 0.0).astype(BF16)
        return carry

    lax.fori_loop(0, half_rows // blk, other_hot, 0)

    def same_target(i, carry):
        rs = pl.ds(pl.multiple_of(i * 64, 64), 64)
        own_row = tgt_buf[0:1].astype(F32)
        same = (tcols_buf[rs, 0:1] == own_row) & (own_row >= 0.0)
        yo[rs, :] = jnp.where(same, b[rs, :], 0.0)
        return carry

    lax.fori_loop(0, T // 64, same_target, 0)

    plane_merge(1 - mz, 1)
    share(st2, col_id, col_peer, 8, ss2, sr2)

    def gram_hot(i, carry):
        rs = columns(i * HALF, HALF)
        lhs = wp[:, rs]
        for n in range(2):
            yx[columns(T + i * HALF, HALF), n * T : (n + 1) * T] = tn(lhs, w[ours, n * T : (n + 1) * T])
        return carry

    lax.fori_loop(0, 2, gram_hot, 0)

    cross_third(1)

    for phase in range(2):
        wait_bytes(ep.at[:, pl.ds(0, HALF)], er.at[phase])

    def gram_cross(i, carry):
        rs = columns(i * HALF, HALF)
        lhs = ep[:, rs]
        for n in range(2):
            yx[rs, n * T : (n + 1) * T] = tn(lhs, w[ours, n * T : (n + 1) * T])
        return carry

    lax.fori_loop(0, 2, gram_cross, 0)

    wait_bytes(st2.at[pl.ds(0, 7)], sr2)
    def line(piece):
        return jnp.concatenate([piece(n)[k : k + 1] for n in range(2) for k in range(2)], axis=1)

    def both(first, second):
        return jnp.where(lax.broadcasted_iota(jnp.int32, (2, T), 0) == 0, first, second)

    merged = [[merge([st2[s * 4 + head * 2 + z, n] for s in range(2) for z in range(2)]) for n in range(2)] for head in range(2)]
    top, tot, pick = (both(*(line(lambda n: merged[head][n][k]) for head in range(2))) for k in range(3))
    lse = top + jnp.log(tot)
    nll = lse - pick
    live = live_buf[0:2]
    weight = jnp.where(lax.broadcasted_iota(jnp.int32, (2, 1), 0) == 0, 1.0, 0.3).astype(F32)
    coef = weight / jnp.maximum(jnp.sum(live, axis=1, keepdims=True), 1.0)
    loss = jnp.sum(coef * jnp.sum(live * nll, axis=1, keepdims=True), axis=0, keepdims=True)
    scale = coef * live
    g = (scale * (jnp.exp(pick - lse) - 1.0)).astype(BF16).astype(F32)
    partner_slot = ms * 4 + (1 - md) * 2 + mz
    origin_p = line(lambda n: st2[partner_slot, n, 6:8])
    origin = orig_buf[0:1]

    def pair(a):
        return (jnp.where(md == 0, a[0:1], a[1:2]), jnp.where(md == 0, a[1:2], a[0:1]))

    scale_o, scale_p = pair(scale)
    lse_o, lse_p = pair(lse)
    g_o, g_p = pair(g)
    s_o = scale_o * jnp.exp(origin - lse_o)
    s_p = scale_p * jnp.exp(origin_p - lse_p)
    vecs = jnp.where(row8 == 0, s_o, jnp.where(row8 == 1, g_o, jnp.where(row8 == 2, 2.0 * s_p, jnp.where(row8 == 3, 2.0 * g_p, 0.0))))
    cols_buf[...] = vecs.T

    cross_wait(0)
    cross_wait(1)

    qb = 64

    def quad(i, carry):
        acc_s, acc_g = carry
        rs = columns(i * qb, qb)
        rt = columns(T + i * qb, qb)
        cols = cols_buf[rs, :]
        so, go, sp, gp = (cols[:, k : k + 1] for k in range(4))
        xx = x2[rs, :]
        lhs = so * y[rs, 0:T] + xx * (sp * yx[rs, 0:T] + gp * yx[rt, 0:T])
        rhs = so * y[rs, T : 2 * T] + go * yo[rs, :] + xx * (sp * yx[rs, T : 2 * T] + gp * yx[rt, T : 2 * T])
        acc_s = acc_s + jnp.sum(lhs.reshape(qb // 8, 8, T), axis=0)
        acc_g = acc_g + jnp.sum(rhs.reshape(qb // 8, 8, T), axis=0)
        return acc_s, acc_g

    zero = jnp.zeros((8, T), F32)
    acc_s, acc_g = lax.fori_loop(0, T // qb, quad, (zero, zero))
    q = jnp.sum(jnp.sum(acc_s * s_o + acc_g * g_o, axis=0, keepdims=True), axis=1, keepdims=True)
    fin1[col_id] = jnp.broadcast_to(q, (8, 128))
    share(fin1, col_id, col_peer, 8, fs1, fr1)

    wait_bytes(h2.at[pl.ds(0, T - 8)], hs)
    wait_bytes(x2.at[pl.ds(0, T - 8)], xs)
    wait_bytes(partner_rows, hps)
    wait_bytes(ep, es)
    wait_bytes(ints1.at[pl.ds(0, 7)], is1)
    wait_bytes(ints2.at[pl.ds(0, 15)], is2)
    wait_bytes(st1.reshape(32, 8, 128).at[pl.ds(0, 30)], ss1)
    wait_bytes(st2.at[pl.ds(0, 7)], ss2)
    nll_own, _ = pair(nll)
    turned = pltpu.roll(jnp.broadcast_to(nll_own, (8, T)), (T - item * 8) % T, 1)

    wait_bytes(fin1.at[pl.ds(0, 7)], fr1)
    fin2[plane_id] = sum(fin1[k] for k in range(8))
    share(fin2, plane_id, plane_peer, 16, fs2, fr2)
    wait_bytes(fin1.at[pl.ds(0, 7)], fs1)
    wait_bytes(fin2.at[pl.ds(0, 15)], fr2)
    norm = jnp.sqrt(jnp.maximum(sum(fin2[k] for k in range(16)), 0.0))
    out_ref[...] = jnp.where(
        row8[:, 0:128] == 0, turned[:, 0:128], jnp.where(row8[:, 0:128] == 1, loss, norm[0:1, 0:1]))
    wait_bytes(fin2.at[pl.ds(0, 15)], fs2)


def local(hidden, embedding, targets, mask):
    dma = pltpu.SemaphoreType.DMA
    vmem, smem = pl.BlockSpec(memory_space=pltpu.VMEM), pl.BlockSpec(memory_space=pltpu.SMEM)
    whole = pl.BlockSpec(memory_space=pl.ANY)
    out = pl.pallas_call(
        kernel,
        out_shape=jax.ShapeDtypeStruct((8, 128), F32),
        in_specs=[whole, whole, smem, smem],
        out_specs=vmem,
        scratch_shapes=[
            pltpu.VMEM((T + 8, D), BF16),
            pltpu.VMEM((VOC, D), BF16),
            pltpu.VMEM((VPAD, T), F32),
            pltpu.VMEM((T, T), F32),
            pltpu.VMEM((T, 8), F32),
            pltpu.VMEM((2, 2, 2, 2, 2, 2, 8, T), F32),
            pltpu.VMEM((VPAD, 2 * T), BF16),
            pltpu.VMEM((VPAD // 2, T), BF16),
            pltpu.VMEM((VPAD // 2, T), BF16),
            pltpu.VMEM((T, 2 * T), F32),
            pltpu.VMEM((T, T), F32),
            pltpu.VMEM((2 * T, 2 * T), F32),
            pltpu.VMEM((8, 8, T), jnp.int32),
            pltpu.VMEM((16, 8, T), jnp.int32),
            pltpu.VMEM((2, 16, 8, 128), F32),
            pltpu.VMEM((8, 2, 8, 128), F32),
            pltpu.VMEM((8, 8, 128), F32),
            pltpu.VMEM((16, 8, 128), F32),
            pltpu.VMEM((8, T), F32),
            pltpu.VMEM((8, T), jnp.int32),
            pltpu.VMEM((8, T), F32),
            pltpu.VMEM((T, 8), F32),
            pltpu.VMEM((T, 8), F32),
            dma,
            dma((SLICES,)),
            dma,
            dma((2 * SLICES, 6)),
            dma,
            dma((2, 5)),
            dma, dma, dma, dma((2,)),
            dma, dma, dma, dma,
            dma, dma((2,)), dma, dma,
            dma, dma, dma, dma,
        ],
        compiler_params=pltpu.CompilerParams(collective_id=0, has_side_effects=True),
        name="heads",
    )(hidden, embedding, targets, mask)
    return (out[0:1, 0:8], out[1, 0], out[2, 0])


def solution(mesh):
    torus = Mesh(mesh.devices.reshape(2, 2, 2, 4, 4), ("s", "d", "zl", "y", "x"))
    group = ("s", "zl", "y", "x")
    return jax.shard_map(
        local,
        mesh=torus,
        in_specs=(P("d", group, None), P(group, None), P("d", group), P("d", group)),
        out_specs=(P("d", group), P(), P()),
        check_vma=False,
    )
```

time: 81.8 us -> 71 us (0.87)
  Pallas kernels: 76.3 us -> 67.7 us
  between operations: 4.16 us -> 0.64 us
  local copies, waits for them, and re-layouts: 1.11 us -> 2.45 us
    pallas_call x1, Pallas kernels: 76.3 us -> 67.7 us  [local(): pl.pallas_call(kernel, out_shape=jax.ShapeDtypeStruct((8, 128), F32), in_...]
    slice x0 -> x2, local copies, waits for them, and re-layouts: none -> 2.45 us  [local(): return (out[0:1, 0:8], out[1, 0], out[2, 0])]
    unnamed x1 -> x0, local copies, waits for them, and re-layouts: 1.11 us -> none
where the time goes in v3:
time: 71 us; the launch traced here: 70.8 us
  Pallas kernels  67.7 us (95%)
  local copies, waits for them, and re-layouts  2.45 us (3%)
    pallas_call x1, Pallas kernels, local(): pl.pallas_call(kernel, out_shape=jax.ShapeDtypeStruct((8, 128), F32), in_...  67.7 us
    slice x2, local copies, waits for them, and re-layouts, local(): return (out[0:1, 0:8], out[1, 0], out[2, 0])  2.45 us

profile of v3, /device:TPU:1, one launch (start us, length us, event | category | flops | bytes accessed | tf_op | source)
XLA Modules:
  0.0 70.8 jit_solution(14739756168439347177)
XLA Ops:
  0.6 67.7 %heads.1 = f32[8,128]{1,0:T(8,128)} custom-call(bf16[1,8,7168]{2,1,0:T(8,128)(2,1)} %hid_ref.1, bf16[1010,7168]{1,0:T(8,128)(2,1)} %emb_ref.1, s32[1,8]{1,0:T(1,128)} %tgt_ref.1, s32[1,8]{1,0:T(1,128)} %mask_ref.1), custom_call_target="tpu_custom_call" | custom-call | tf_op jit(solution)/shard_map/heads/pallas_call | solution.py:514
  68.4 1.3 %fusion = (f32[1,1]{1,0:T(1,128)}, f32[1,1]{1,0:T(1,128)}) fusion(f32[8,128]{1,0:T(8,128)} %heads.1), kind=kLoop, calls=%fused_computation | loop fusion | bytes 16 | tf_op jit(solution)/shard_map/slice | solution.py:557
  69.6 1.2 %slice.9 = f32[1,8]{1,0:T(1,128)} slice(f32[8,128]{1,0:T(8,128)} %heads.1), slice={[0:1], [0:8]} | slice | bytes 64 | tf_op jit(solution)/shard_map/slice | solution.py:557

commit v4 on v3

--- a/solution.py
+++ b/solution.py
@@ -19,10 +19,13 @@
 HALF = T // 2
 SUBS = 4
 SUBW = WIDTH // SUBS
+DIRECT = 7
+DOUBLED = 2 * SLICES - DIRECT
 LEAD = 2
-LAG = 2
-FIRST = SLICES + LEAD - 4 * LAG
-TURN_A = SLICES + LEAD
+LAG = 3
+SKIP = 3
+TURN_R = SKIP + 3 * LAG + 1
+TURN_A = TURN_R + SLICES - 1 - DIRECT
 NEUTRAL = -1e30
 SHIFT = 13.862943611198906
 CYCLE = (5, 3, 4, 2)
@@ -31,9 +34,9 @@
 def kernel(
     hid_ref, emb_ref, tgt_ref, mask_ref, out_ref,
     hx, emb, l, b, xt, xall, w, wp, ep, y, yo, yx,
-    ints1, ints2, st1, st2, fin1, fin2, live_buf, tgt_buf, orig_buf, tcols_buf, cols_buf,
+    ints1, ints2, ints3, st1, st2, fin1, fin2, live_buf, tgt_buf, orig_buf, tcols_buf, cols_buf,
     hid_sem, emb_sem, hs, hr, xs, xr, hps, hpr, es, er,
-    is1, ir1, is2, ir2, ss1, sr1, ss2, sr2, fs1, fr1, fs2, fr2,
+    is1, ir1, is2, ir2, is3, ir3, ss1, sr1, ss2, sr2, fs1, fr1, fs2, fr2,
 ):
     ms, md, mz, my, mx = (lax.axis_index(a) for a in ("s", "d", "zl", "y", "x"))
     zz = md * 2 + mz
@@ -91,13 +94,14 @@
     for c in range(SLICES):
         emb_copy(c).start()
 
-    lane = lax.broadcasted_iota(jnp.int32, (8, T), 1)
     row8 = lax.broadcasted_iota(jnp.int32, (8, T), 0)
-    ints = jnp.zeros((8, T), jnp.int32)
+    row16 = lax.broadcasted_iota(jnp.int32, (16, 128), 0)
+    lane = lax.broadcasted_iota(jnp.int32, (16, 128), 1)
+    ints = jnp.zeros((16, 128), jnp.int32)
     for i in range(8):
-        here = lane == item * 8 + i
-        ints = jnp.where(here & (row8 == md), tgt_ref[0, i], ints)
-        ints = jnp.where(here & (row8 == 2 + md), mask_ref[0, i], ints)
+        here = lane == (item % 16) * 8 + i
+        ints = jnp.where(here & (row16 == md * 4 + item // 16), tgt_ref[0, i], ints)
+        ints = jnp.where(here & (row16 == 8 + md * 4 + item // 16), mask_ref[0, i], ints)
     ints1[col_id] = ints
     l[...] = jnp.zeros_like(l)
     b[...] = jnp.zeros_like(b)
@@ -116,8 +120,8 @@
     def columns(start, width):
         return pl.ds(pl.multiple_of(start, width), width)
 
-    def slice_wait(unit, c, stage, items):
-        wait_bytes(h2.at[pl.ds(0, 8 * items), columns(c * WIDTH, WIDTH)], hr.at[unit, stage])
+    def slice_wait(unit, stage, items):
+        wait_bytes(h2.at[pl.ds(0, 8 * items), pl.ds(0, WIDTH)], hr.at[unit, stage])
 
     def x_peer(k):
         return {"x": (mx + k) % 4}
@@ -132,18 +136,26 @@
             for k in (2, 1, 3):
                 send(where, where, hs, hr.at[c, stage], (second if stage else first)(k))
 
-    def cube_send(c, step):
+    def place(unit):
+        phase = unit // SLICES
+        return unit - phase * SLICES, mz + phase * (1 - 2 * mz), phase
+
+    def cube_send(unit, step):
+        c, plane, _ = place(unit)
         for sub in range(SUBS):
             dims = [CYCLE[(sub + k) % 4] for k in range(4)]
-            where = h.at[box(dims[:step], columns(c * WIDTH + sub * SUBW, SUBW), 1 - mz)]
-            send(where, where, hs, hr.at[SLICES + c, 1 + step], partner[dims[step]])
-
-    def core_send(unit, c, plane, stage):
+            where = h.at[box(dims[:step], columns(c * WIDTH + sub * SUBW, SUBW), plane)]
+            send(where, where, hs, hr.at[unit, 1 + step], partner[dims[step]])
+
+    def core_send(unit):
+        c, plane, _ = place(unit)
         where = h.at[box((2, 3, 4, 5), columns(c * WIDTH, WIDTH), plane)]
-        send(where, where, hs, hr.at[unit, stage], core)
-
-    for c in range(SLICES):
+        send(where, where, hs, hr.at[unit, 5], core)
+
+    for c in range(DIRECT):
         direct_send(c, 0)
+    for c in range(DIRECT, SLICES):
+        cube_send(c, 0)
     send(h.at[mine], partner_rows, hps, hpr, {"d": 1 - md})
     for c in range(SLICES):
         where = h.at[(*mine, slice(None), columns(c * WIDTH, WIDTH))]
@@ -257,59 +269,65 @@
         send(w.at[theirs, ls], ep.at[:, ls], es, er.at[phase], {"d": 1 - md})
 
     def body(i, carry):
-        @pl.when(i < SLICES)
-        def _():
-            slice_wait(i, i, 0, 3)
+        @pl.when(i < DIRECT)
+        def _():
+            slice_wait(i, 0, 3)
             direct_send(i, 1)
 
         c = i - LEAD
 
-        @pl.when((c >= 0) & (c < SLICES))
-        def _():
-            slice_wait(c, c, 1, 12)
-            core_send(c, c, mz, 2)
-
-        c4 = i - FIRST - 4 * LAG
-
-        @pl.when((c4 >= 0) & (c4 < SLICES))
-        def _():
-            slice_wait(SLICES + c4, c4, 4, 8)
-            core_send(SLICES + c4, c4, 1 - mz, 5)
-
-        for step in (3, 2, 1, 0):
-            c = i - FIRST - step * LAG
-
-            @pl.when((c >= 0) & (c < SLICES))
-            def _(c=c, step=step):
-                slice_wait(SLICES + c, c, step, 2 ** max(step - 1, 0))
-                cube_send(c, step)
-
-        @pl.when(i == 5)
+        @pl.when((c >= 0) & (c < DIRECT))
+        def _():
+            slice_wait(c, 1, 12)
+            core_send(c)
+
+        r4 = i - 3 * LAG - SKIP
+
+        @pl.when((r4 >= 0) & (r4 < DOUBLED))
+        def _():
+            slice_wait(DIRECT + r4, 4, 8)
+            core_send(DIRECT + r4)
+
+        for step in (3, 2, 1):
+            r = i - (step - 1) * LAG - SKIP
+
+            @pl.when((r >= 0) & (r < DOUBLED))
+            def _(r=r, step=step):
+                slice_wait(DIRECT + r, step, 2 ** (step - 1))
+                cube_send(DIRECT + r, step)
+
+        unit0 = DIRECT + i + LAG - SKIP
+
+        @pl.when((unit0 >= SLICES) & (unit0 < 2 * SLICES))
+        def _():
+            slice_wait(unit0, 0, 1)
+            cube_send(unit0, 0)
+
+        @pl.when(i == 4)
         def _():
             wait_bytes(ints1.at[pl.ds(0, 7)], ir1)
-            ints2[plane_id] = sum(ints1[k] for k in range(8))
-            share(ints2, plane_id, plane_peer, 16, is2, ir2)
-
-        u = i - LEAD - 1
-
-        @pl.when(u == 0)
+            ints2[mx] = sum(ints1[k] for k in range(8))
+            share(ints2, mx, x_peer, 4, is2, ir2)
+
+        @pl.when(i == 7)
+        def _():
+            wait_bytes(ints2.at[pl.ds(0, 3)], ir2)
+            ints3[my] = sum(ints2[k] for k in range(4))
+            share(ints3, my, y_peer, 4, is3, ir3)
+
+        @pl.when(i == LEAD + 1)
         def _():
             wait_bytes(partner_rows, hpr)
 
-        @pl.when(u >= 0)
-        def _():
-            phase = u // SLICES
-            c = u - phase * SLICES
-            n = mz + phase * (1 - 2 * mz)
+        @pl.when(((i > LEAD) & (i <= LEAD + DIRECT)) | (i >= TURN_R))
+        def _():
+            unit = jnp.where(i >= TURN_R, i - TURN_R + DIRECT, i - LEAD - 1)
+            c, n, phase = place(unit)
+            slice_wait(unit, 5, 16)
 
             @pl.when(phase == 0)
             def _():
-                slice_wait(c, c, 2, 16)
                 emb_copy(c).wait()
-
-            @pl.when(phase == 1)
-            def _():
-                slice_wait(SLICES + c, c, 5, 16)
 
             cs, ls = columns(c * WIDTH, WIDTH), columns(n * HALF, HALF)
             hn = h2[ls, cs]
@@ -323,20 +341,37 @@
 
         @pl.when(i == TURN_A)
         def _():
-            wait_bytes(ints2.at[pl.ds(0, 15)], ir2)
-            ints = sum(ints2[k] for k in range(16))
+            wait_bytes(ints3.at[pl.ds(0, 3)], ir3)
+            ints = sum(ints3[k] for k in range(4))
             first_id = (ms * 32 + mz * 16 + my * 4 + mx) * VOC
-            local_t = ints[0:2] - first_id
-            local_t = jnp.where(local_t < VOC, local_t, -1)
-            tgt_buf[0:1] = jnp.where(md == 0, local_t[0:1], local_t[1:2])
-            tgt_buf[1:2] = jnp.where(md == 0, local_t[1:2], local_t[0:1])
-            live_buf[0:2] = ints[2:4].astype(F32)
+            lines = [
+                jnp.concatenate([ints[4 * k + part : 4 * k + part + 1] for part in range(4)], axis=1)
+                for k in range(4)
+            ]
+            local_t = [jnp.where(line - first_id < VOC, line - first_id, -1) for line in lines[:2]]
+            tgt_buf[0:1] = jnp.where(md == 0, local_t[0], local_t[1])
+            tgt_buf[1:2] = jnp.where(md == 0, local_t[1], local_t[0])
+            live_buf[0:1] = lines[2].astype(F32)
+            live_buf[1:2] = lines[3].astype(F32)
             tail = l[VOC - 2 : VPAD]
             tail_row = lax.broadcasted_iota(jnp.int32, tail.shape, 0)
             l[VOC - 2 : VPAD] = jnp.where(tail_row < 2, tail, NEUTRAL)
             finish_half(mz, 0)
             exchange(mz, 0)
 
+        @pl.when(i == TURN_A + 2)
+        def _():
+            other_t = tgt_buf[1:2]
+            rows_full = lax.broadcasted_iota(jnp.int32, (blk, T), 0)
+
+            def other_hot(i, carry):
+                at = pl.multiple_of(i * blk, blk)
+                hit = (rows_full + (at + md * half_rows)) == other_t
+                wp[pl.ds(at, blk), :] = jnp.where(hit, 1.0, 0.0).astype(BF16)
+                return carry
+
+            lax.fori_loop(0, half_rows // blk, other_hot, 0)
+
         @pl.when(i == TURN_A + 3)
         def _():
             cross_second(0)
@@ -351,7 +386,7 @@
 
         return carry
 
-    lax.fori_loop(0, 2 * SLICES + LEAD + 1, body, 0)
+    lax.fori_loop(0, TURN_R + DOUBLED, body, 0)
 
     finish_half(1 - mz, 1)
     exchange(1 - mz, 1)
@@ -359,12 +394,11 @@
     own_cols, late_cols = columns(mz * HALF, HALF), columns((1 - mz) * HALF, HALF)
 
     def late_b(c, carry):
-        cs = columns(c * WIDTH, WIDTH)
+        cs = columns(c * (D // 2), D // 2)
         b[:, late_cols] += nt(h2[:, cs], h2[late_cols, cs])
         return carry
 
-    lax.fori_loop(0, SLICES, late_b, 0)
-    cross_second(1)
+    lax.fori_loop(0, 2, late_b, 0)
     b[late_cols, own_cols] = b[own_cols, late_cols].T
 
     tgt_rows = jnp.where(row8 < 2, jnp.broadcast_to(tgt_buf[0:1], (8, T)), 0).astype(F32)
@@ -382,17 +416,7 @@
         return carry
 
     lax.fori_loop(0, 2, gram_own, 0)
-
-    other_t = tgt_buf[1:2]
-    rows_full = lax.broadcasted_iota(jnp.int32, (blk, T), 0)
-
-    def other_hot(i, carry):
-        at = pl.multiple_of(i * blk, blk)
-        hit = (rows_full + (at + md * half_rows)) == other_t
-        wp[pl.ds(at, blk), :] = jnp.where(hit, 1.0, 0.0).astype(BF16)
-        return carry
-
-    lax.fori_loop(0, half_rows // blk, other_hot, 0)
+    cross_second(1)
 
     def same_target(i, carry):
         rs = pl.ds(pl.multiple_of(i * 64, 64), 64)
@@ -417,17 +441,16 @@
 
     cross_third(1)
 
-    for phase in range(2):
-        wait_bytes(ep.at[:, pl.ds(0, HALF)], er.at[phase])
-
-    def gram_cross(i, carry):
-        rs = columns(i * HALF, HALF)
+    def gram_cross(half):
+        rs = columns(half * HALF, HALF)
         lhs = ep[:, rs]
         for n in range(2):
             yx[rs, n * T : (n + 1) * T] = tn(lhs, w[ours, n * T : (n + 1) * T])
-        return carry
-
-    lax.fori_loop(0, 2, gram_cross, 0)
+
+    wait_bytes(ep.at[:, pl.ds(0, HALF)], er.at[0])
+    gram_cross(mz)
+    wait_bytes(ep.at[:, pl.ds(0, HALF)], er.at[1])
+    gram_cross(1 - mz)
 
     wait_bytes(st2.at[pl.ds(0, 7)], sr2)
     def line(piece):
@@ -490,7 +513,8 @@
     wait_bytes(partner_rows, hps)
     wait_bytes(ep, es)
     wait_bytes(ints1.at[pl.ds(0, 7)], is1)
-    wait_bytes(ints2.at[pl.ds(0, 15)], is2)
+    wait_bytes(ints2.at[pl.ds(0, 3)], is2)
+    wait_bytes(ints3.at[pl.ds(0, 3)], is3)
     wait_bytes(st1.reshape(32, 8, 128).at[pl.ds(0, 30)], ss1)
     wait_bytes(st2.at[pl.ds(0, 7)], ss2)
     nll_own, _ = pair(nll)
@@ -529,8 +553,9 @@
             pltpu.VMEM((T, 2 * T), F32),
             pltpu.VMEM((T, T), F32),
             pltpu.VMEM((2 * T, 2 * T), F32),
-            pltpu.VMEM((8, 8, T), jnp.int32),
-            pltpu.VMEM((16, 8, T), jnp.int32),
+            pltpu.VMEM((8, 16, 128), jnp.int32),
+            pltpu.VMEM((4, 16, 128), jnp.int32),
+            pltpu.VMEM((4, 16, 128), jnp.int32),
             pltpu.VMEM((2, 16, 8, 128), F32),
             pltpu.VMEM((8, 2, 8, 128), F32),
             pltpu.VMEM((8, 8, 128), F32),
@@ -547,7 +572,7 @@
             dma,
             dma((2, 5)),
             dma, dma, dma, dma((2,)),
-            dma, dma, dma, dma,
+            dma, dma, dma, dma, dma, dma,
             dma, dma((2,)), dma, dma,
             dma, dma, dma, dma,
         ],

time: 71 us -> 68.5 us (0.965)
  Pallas kernels: 67.7 us -> 65.2 us
    pallas_call x1, Pallas kernels: 67.7 us -> 65.2 us  [local(): pl.pallas_call(kernel, out_shape=jax.ShapeDtypeStruct((8, 128), F32), in_...]
where the time goes in v4:
time: 68.5 us; the launch traced here: 68.2 us
  Pallas kernels  65.2 us (95%)
  local copies, waits for them, and re-layouts  2.45 us (4%)
    pallas_call x1, Pallas kernels, local(): pl.pallas_call(kernel, out_shape=jax.ShapeDtypeStruct((8, 128), F32), in_...  65.2 us
    slice x2, local copies, waits for them, and re-layouts, local(): return (out[0:1, 0:8], out[1, 0], out[2, 0])  2.45 us

profile of v4, /device:TPU:1, one launch (start us, length us, event | category | flops | bytes accessed | tf_op | source)
XLA Modules:
  0.0 68.2 jit_solution(5373148578421558806)
XLA Ops:
  0.6 65.2 %heads.1 = f32[8,128]{1,0:T(8,128)} custom-call(bf16[1,8,7168]{2,1,0:T(8,128)(2,1)} %hid_ref.1, bf16[1010,7168]{1,0:T(8,128)(2,1)} %emb_ref.1, s32[1,8]{1,0:T(1,128)} %tgt_ref.1, s32[1,8]{1,0:T(1,128)} %mask_ref.1), custom_call_target="tpu_custom_call" | custom-call | tf_op jit(solution)/shard_map/heads/pallas_call | solution.py:538
  65.8 1.3 %fusion = (f32[1,1]{1,0:T(1,128)}, f32[1,1]{1,0:T(1,128)}) fusion(f32[8,128]{1,0:T(8,128)} %heads.1), kind=kLoop, calls=%fused_computation | loop fusion | bytes 16 | tf_op jit(solution)/shard_map/slice | solution.py:582
  67.1 1.2 %slice.9 = f32[1,8]{1,0:T(1,128)} slice(f32[8,128]{1,0:T(8,128)} %heads.1), slice={[0:1], [0:8]} | slice | bytes 64 | tf_op jit(solution)/shard_map/slice | solution.py:582

commit v5 on v4

--- a/solution.py
+++ b/solution.py
@@ -156,10 +156,11 @@
         direct_send(c, 0)
     for c in range(DIRECT, SLICES):
         cube_send(c, 0)
-    send(h.at[mine], partner_rows, hps, hpr, {"d": 1 - md})
     for c in range(SLICES):
         where = h.at[(*mine, slice(None), columns(c * WIDTH, WIDTH))]
         send(where, where, hs, hr.at[SLICES + c, 0], other_plane)
+        if c == 2:
+            send(h.at[mine], partner_rows, hps, hpr, {"d": 1 - md})
     share(ints1, col_id, col_peer, 8, is1, ir1)
 
     def nt(lhs, rhs):
@@ -230,7 +231,10 @@
             w[pl.ds(at, blk), columns(T + n * HALF, HALF)] = jnp.where(hit, 1.0, 0.0).astype(BF16)
             return total + jnp.sum(e.reshape(groups, 8, HALF), axis=0)
 
-        total = lax.fori_loop(0, VPAD // blk, exp_body, jnp.zeros((8, HALF), F32))
+        count = half_rows // blk
+        total = lax.fori_loop((1 - md) * count, (2 - md) * count, exp_body, jnp.zeros((8, HALF), F32))
+        send(w.at[theirs, ls], ep.at[:, ls], es, er.at[phase], {"d": 1 - md})
+        total = lax.fori_loop(md * count, (1 + md) * count, exp_body, total)
         total = jnp.sum(total, axis=0, keepdims=True)
         st1[phase, plane_id] = tile(origin, total, chosen)
         orig_buf[0:1, ls] = origin
@@ -264,10 +268,6 @@
         st2[col_id, n, 6:7] = own_origin[:, 0:128]
         st2[col_id, n, 7:8] = own_origin[:, 128:256]
 
-    def exchange(n, phase):
-        ls = columns(n * HALF, HALF)
-        send(w.at[theirs, ls], ep.at[:, ls], es, er.at[phase], {"d": 1 - md})
-
     def body(i, carry):
         @pl.when(i < DIRECT)
         def _():
@@ -331,12 +331,17 @@
 
             cs, ls = columns(c * WIDTH, WIDTH), columns(n * HALF, HALF)
             hn = h2[ls, cs]
-            l[0:VOC, ls] += nt(emb[:, cs], hn)
             xt[ls, :] += nt(hn, partner_rows[:, cs])
 
             @pl.when(phase == 0)
             def _():
-                b[ls, ls] += nt(hn, hn)
+                part = nt(jnp.concatenate([hn, emb[:, cs]], axis=0), hn)
+                b[ls, ls] += part[:HALF]
+                l[0:VOC, ls] += part[HALF:]
+
+            @pl.when(phase == 1)
+            def _():
+                l[0:VOC, ls] += nt(emb[:, cs], hn)
 
 
         @pl.when(i == TURN_A)
@@ -357,7 +362,6 @@
             tail_row = lax.broadcasted_iota(jnp.int32, tail.shape, 0)
             l[VOC - 2 : VPAD] = jnp.where(tail_row < 2, tail, NEUTRAL)
             finish_half(mz, 0)
-            exchange(mz, 0)
 
         @pl.when(i == TURN_A + 2)
         def _():
@@ -389,7 +393,6 @@
     lax.fori_loop(0, TURN_R + DOUBLED, body, 0)
 
     finish_half(1 - mz, 1)
-    exchange(1 - mz, 1)
 
     own_cols, late_cols = columns(mz * HALF, HALF), columns((1 - mz) * HALF, HALF)
 
@@ -415,8 +418,9 @@
         y[rs, T : 2 * T] = tn(lhs, w[:, T : 2 * T]) * (2.0 * bb)
         return carry
 
-    lax.fori_loop(0, 2, gram_own, 0)
+    gram_own(mz, 0)
     cross_second(1)
+    gram_own(1 - mz, 0)
 
     def same_target(i, carry):
         rs = pl.ds(pl.multiple_of(i * 64, 64), 64)
@@ -529,6 +533,12 @@
     out_ref[...] = jnp.where(
         row8[:, 0:128] == 0, turned[:, 0:128], jnp.where(row8[:, 0:128] == 1, loss, norm[0:1, 0:1]))
     wait_bytes(fin2.at[pl.ds(0, 15)], fs2)
+
+
+def parted(all_ref, nll_ref, loss_ref, norm_ref):
+    nll_ref[...] = all_ref[0:1, 0:8]
+    loss_ref[...] = all_ref[1:2, 0:1]
+    norm_ref[...] = all_ref[2:3, 0:1]
 
 
 def local(hidden, embedding, targets, mask):
@@ -579,7 +589,15 @@
         compiler_params=pltpu.CompilerParams(collective_id=0, has_side_effects=True),
         name="heads",
     )(hidden, embedding, targets, mask)
-    return (out[0:1, 0:8], out[1, 0], out[2, 0])
+    one = pl.BlockSpec(memory_space=pltpu.VMEM)
+    nll, loss, norm = pl.pallas_call(
+        parted,
+        out_shape=(jax.ShapeDtypeStruct((1, 8), F32), jax.ShapeDtypeStruct((1, 1), F32), jax.ShapeDtypeStruct((1, 1), F32)),
+        in_specs=[one],
+        out_specs=(one, one, one),
+        name="parted",
+    )(out)
+    return (nll, loss[0, 0], norm[0, 0])
 
 
 def solution(mesh):

time: 68.5 us -> 66.9 us (0.977)
  local copies, waits for them, and re-layouts: 2.45 us -> 0 us
  Pallas kernels: 65.2 us -> 66.1 us
    slice x2 -> x0, local copies, waits for them, and re-layouts: 2.45 us -> none  [local(): return (out[0:1, 0:8], out[1, 0], out[2, 0])]
    pallas_call x0 -> x1, Pallas kernels: none -> 1.19 us  [local(): pl.pallas_call(parted, out_shape=(jax.ShapeDtypeStruct((1, 8), F32), jax....]
where the time goes in v5:
time: 66.9 us; the launch traced here: 66.7 us
  Pallas kernels  66.1 us (99%)
    pallas_call x1, Pallas kernels, local(): pl.pallas_call(kernel, out_shape=jax.ShapeDtypeStruct((8, 128), F32), in_...  64.9 us

profile of v5, /device:TPU:1, one launch (start us, length us, event | category | flops | bytes accessed | tf_op | source)
XLA Modules:
  0.0 66.7 jit_solution(5267771661043216228)
XLA Ops:
  0.6 64.9 %heads.1.all_ref = f32[8,128]{1,0:T(8,128)} custom-call(bf16[1,8,7168]{2,1,0:T(8,128)(2,1)} %hid_ref.1, bf16[1010,7168]{1,0:T(8,128)(2,1)} %emb_ref.1, s32[1,8]{1,0:T(1,128)} %tgt_ref.1, s32[1,8]{1,0:T(1,128)} %mask_ref.1), custom_call_target="tpu_custom_call" | custom-call | tf_op jit(solution)/shard_map/heads/pallas_call | solution.py:548
  65.5 1.2 %parted.1 = (f32[1,8]{1,0:T(1,128)}, f32[1,1]{1,0:T(1,128)}, f32[1,1]{1,0:T(1,128)}) custom-call(f32[8,128]{1,0:T(8,128)} %heads.1.all_ref), custom_call_target="tpu_custom_call" | custom-call | tf_op jit(solution)/shard_map/parted/pallas_call | solution.py:593

commit v6 on v5

--- a/solution.py
+++ b/solution.py
@@ -21,7 +21,7 @@
 SUBW = WIDTH // SUBS
 DIRECT = 7
 DOUBLED = 2 * SLICES - DIRECT
-LEAD = 2
+LEAD = 3
 LAG = 3
 SKIP = 3
 TURN_R = SKIP + 3 * LAG + 1
@@ -331,10 +331,10 @@
 
             cs, ls = columns(c * WIDTH, WIDTH), columns(n * HALF, HALF)
             hn = h2[ls, cs]
-            xt[ls, :] += nt(hn, partner_rows[:, cs])
 
             @pl.when(phase == 0)
             def _():
+                xt[ls, :] += nt(hn, partner_rows[:, cs])
                 part = nt(jnp.concatenate([hn, emb[:, cs]], axis=0), hn)
                 b[ls, ls] += part[:HALF]
                 l[0:VOC, ls] += part[HALF:]
@@ -342,6 +342,7 @@
             @pl.when(phase == 1)
             def _():
                 l[0:VOC, ls] += nt(emb[:, cs], hn)
+                xt[ls, :] += nt(hn, partner_rows[:, cs])
 
 
         @pl.when(i == TURN_A)

time: 66.9 us -> 63.8 us (0.954)
  Pallas kernels: 66.1 us -> 63 us
    pallas_call x1, Pallas kernels: 64.9 us -> 61.8 us  [local(): pl.pallas_call(kernel, out_shape=jax.ShapeDtypeStruct((8, 128), F32), in_...]
where the time goes in v6:
time: 63.8 us; the launch traced here: 63.6 us
  Pallas kernels  63 us (99%)
  between operations  0.64 us (1%)
    pallas_call x1, Pallas kernels, local(): pl.pallas_call(kernel, out_shape=jax.ShapeDtypeStruct((8, 128), F32), in_...  61.8 us

profile of v6, /device:TPU:1, one launch (start us, length us, event | category | flops | bytes accessed | tf_op | source)
XLA Modules:
  0.0 63.6 jit_solution(10556816391686759011)
XLA Ops:
  0.6 61.8 %heads.1.all_ref = f32[8,128]{1,0:T(8,128)} custom-call(bf16[1,8,7168]{2,1,0:T(8,128)(2,1)} %hid_ref.1, bf16[1010,7168]{1,0:T(8,128)(2,1)} %emb_ref.1, s32[1,8]{1,0:T(1,128)} %tgt_ref.1, s32[1,8]{1,0:T(1,128)} %mask_ref.1), custom_call_target="tpu_custom_call" | custom-call | tf_op jit(solution)/shard_map/heads/pallas_call | solution.py:549
  62.5 1.2 %parted.1 = (f32[1,8]{1,0:T(1,128)}, f32[1,1]{1,0:T(1,128)}, f32[1,1]{1,0:T(1,128)}) custom-call(f32[8,128]{1,0:T(8,128)} %heads.1.all_ref), custom_call_target="tpu_custom_call" | custom-call | tf_op jit(solution)/shard_map/parted/pallas_call | solution.py:594
